TPU v7x, 256 devices: a whole 4x4x8 slice. The times are simulated.
256 devices in a mesh: variant: 8 (over y, x_lo), mp: 32 (over x_hi, z, core).
Axes of the slice: x: 4 (x_hi: 2, x_lo: 2; x = x_hi * 2 + x_lo), y: 4, z: 8, core: 2. Of those that a mesh axis runs over, the one named last changes fastest.
Arguments:
- positions: bfloat16 [131072, 1024], P(('variant', 'mp')), may hold values from -6 to 6
- game_counts: int32 [256], P(('variant', 'mp')), may hold values from 384 to 512
- block_variant: int32 [1024], P(('variant', 'mp')), may hold values from 0 to 7, as said below
- norm_gain: float32 [8, 1024], P('variant'), may hold values from 0.25 to 1.75
- up_weight: bfloat16 [8, 1024, 2048], P('variant', 'mp'), may hold values from -0.1875 to 0.1875
- down_weight: bfloat16 [8, 2048, 1024], P('variant', 'mp'), may hold values from -0.125 to 0.125
- final_gain: float32 [8, 1024], P('variant'), may hold values from 0.25 to 1.75
- value_weight: float32 [8, 1024], P('variant'), may hold values from -0.1875 to 0.1875
- policy_weight: bfloat16 [1024, 2336], P(('variant', 'mp')), may hold values from -0.1875 to 0.1875
Outputs:
- policy: bfloat16 [131072, 2336], P(('variant', 'mp'))
- value: float32 [131072], P(('variant', 'mp'))
Inputs may be any that keep to these rules, and one draw needn't show every extreme that they name: `block_variant`: the 4 blocks of one device name 4 different variants.
All inputs are finite; a program needn't handle non-finite values.
Results may differ from a plain program's by a relative error of at most 0.0056.
Values may be sent and summed in bfloat16 or wider, within the bound.
A program may use at most 128 MiB of HBM per device.

v0:
```python
import jax
import jax.numpy as jnp
from jax import lax
from jax.sharding import PartitionSpec as P

D = 1024
BLOCK = 128


def laid_out(parts, dim):
    parts = jnp.moveaxis(parts, 0, dim)
    shape = parts.shape
    return parts.reshape(*shape[:dim], shape[dim] * shape[dim + 1], *shape[dim + 2 :])


def from_everyone(x, axis):
    size = lax.axis_size(axis)
    return lax.all_to_all(jnp.broadcast_to(x[None], (size, *x.shape)), axis, 0, 0, tiled=True)


def gather_directly(x, axis, dim):
    return laid_out(from_everyone(x, axis), dim)


def one_gather(arrays, axis, dims):
    ravelled = jnp.concatenate([a.reshape(-1) for a in arrays])
    lines, at, gathered = (lax.all_gather(ravelled, axis), 0, [])
    for a, dim in zip(arrays, dims):
        parts = lines[:, at : at + a.size].reshape(-1, *a.shape)
        gathered.append(laid_out(parts, dim))
        at += a.size
    return tuple(gathered)


def cut_along(x, dim, size):
    shape = x.shape
    parts = x.reshape(*shape[:dim], size, shape[dim] // size, *shape[dim + 1 :])
    return jnp.moveaxis(parts, dim, 0)


def cut_rows(length, count):
    unit = 8 if length >= 8 * count else 1
    return [length // unit * k // count * unit for k in range(1, count)]


def several_exchanges(x, axis, pieces, split_dim, concat_dim):
    parts = cut_along(x, split_dim, lax.axis_size(axis))
    cut = max(range(1, max(2, parts.ndim - 1)), key=lambda d: parts.shape[d])
    gathered = []
    for share in jnp.split(parts, cut_rows(parts.shape[cut], pieces), axis=cut):
        if share.size:
            gathered.append(lax.all_to_all(share, axis, split_axis=0, concat_axis=0, tiled=True))
    return laid_out(jnp.concatenate(gathered, axis=cut), concat_dim)


def rms_scale(values, scale_gain):
    mean_square = jnp.mean(values * values, axis=-1, keepdims=True)
    return values * lax.rsqrt(mean_square + 1e-06) * scale_gain


def row_adder(operand, shard_rows):
    return jnp.dot(operand, shard_rows, preferred_element_type=jnp.float32)


def network_rows(values, upward_fn, downward_fn, norm_gain, final_gain):
    normed = rms_scale(values, norm_gain).astype(jnp.bfloat16)
    upward = upward_fn(normed)
    active = jax.nn.gelu(upward, approximate=True).astype(jnp.bfloat16)
    downward = downward_fn(active)
    return rms_scale(values + downward, final_gain)


def policy_logits(hidden_rows, policy_weight):
    group_rows = gather_directly(policy_weight, "mp", 0)
    summed = row_adder(hidden_rows, lax.all_gather(group_rows, "variant", axis=0, tiled=True))
    return summed.astype(jnp.bfloat16)


def local(
    positions,
    game_counts,
    block_variant,
    norm_gain,
    up_weight,
    down_weight,
    final_gain,
    value_weight,
    policy_weight,
):
    variants = lax.axis_size("variant")
    block_count = block_variant.shape[0]
    games_here = positions.shape[0]
    local_blocks = positions.reshape(block_count, BLOCK, D)
    starts = jnp.arange(block_count, dtype=jnp.int32) * BLOCK
    block_live = jnp.clip(game_counts[0] - starts, 0, BLOCK)
    selector = block_variant[None, :] == jnp.arange(variants, dtype=jnp.int32)[:, None]
    selector_b = selector.astype(jnp.bfloat16)
    outgoing = jnp.einsum(
        "jb,brd->jrd", selector_b, local_blocks, preferred_element_type=jnp.float32
    ).astype(jnp.bfloat16)
    out_live = jnp.sum(jnp.where(selector, block_live[None, :], 0), axis=1)
    incoming, in_live = (
        lax.all_to_all(outgoing, "variant", split_axis=0, concat_axis=0, tiled=True),
        lax.all_to_all(out_live, "variant", split_axis=0, concat_axis=0, tiled=True),
    )
    slot_rows = variants * BLOCK
    up_whole, down_whole = one_gather((up_weight[0], down_weight[0]), "mp", (0, 0))

    def compute_slot(block_rows):
        return network_rows(
            block_rows.astype(jnp.float32),
            lambda normed: jnp.dot(normed, up_whole, preferred_element_type=jnp.float32),
            lambda active: jnp.dot(active, down_whole, preferred_element_type=jnp.float32),
            norm_gain[0],
            final_gain[0],
        )

    def empty_slot(block_rows):
        return jnp.zeros((BLOCK, D), jnp.float32)

    def one_slot(slot_entry):
        return lax.cond(slot_entry[1] > 0, compute_slot, empty_slot, slot_entry[0])

    hidden = lax.map(one_slot, (incoming, in_live)).reshape(slot_rows, D)
    estimate = jnp.tanh(jnp.sum(hidden * value_weight[0], axis=-1)).reshape(variants, BLOCK)
    hidden_b = hidden.astype(jnp.bfloat16)
    returned, returned_value = (
        several_exchanges(hidden_b.reshape(variants, BLOCK, D), "variant", 2, 0, 0),
        several_exchanges(estimate.astype(jnp.bfloat16), "variant", 2, 0, 0).astype(estimate.dtype),
    )
    own_hidden = jnp.einsum(
        "jb,jrd->brd", selector_b, returned, preferred_element_type=jnp.float32
    ).astype(jnp.bfloat16)
    own_logits = policy_logits(own_hidden.reshape(games_here, D), policy_weight)
    own_value = jnp.sum(
        jnp.where(selector[:, :, None], returned_value[:, None, :], 0.0), axis=0
    ).reshape(games_here)
    row_live = jnp.arange(games_here, dtype=jnp.int32) < game_counts[0]
    policy = jnp.where(row_live[:, None], own_logits, jnp.zeros((), jnp.bfloat16))
    value = jnp.where(row_live, own_value, jnp.zeros((), jnp.float32))
    return (policy, value)


def solution(mesh):
    in_specs = (
        P(("variant", "mp"), None),
        P(("variant", "mp")),
        P(("variant", "mp")),
        P("variant", None),
        P("variant", "mp", None),
        P("variant", "mp", None),
        P("variant", None),
        P("variant", None),
        P(("variant", "mp"), None),
    )
    out_specs = (P(("variant", "mp"), None), P(("variant", "mp")))
    return jax.shard_map(local, mesh=mesh, in_specs=in_specs, out_specs=out_specs, check_vma=False)
```

profile of v0, /device:TPU:8, one launch (start us, length us, event | category | flops | bytes accessed | tf_op | source)
XLA Modules:
  0.0 293.5 jit_solution(9887362912586621010)
XLA Ops:
  11.4 10.4 %all_to_all.37 = s32[8,1,1]{2,1,0:T(1,128)S(1)} all-to-all(s32[8,1,1]{2,1,0:T(1,128)S(1)} %copy.35), channel_id=1, replica_groups=mesh['variant'=8,'mp'=32] {'variant'}, dimensions={0} | all-to-all | bytes 64 | tf_op jit(solution)/shard_map/all_to_all | solution.py:104
  21.8 1.7 broadcast_in_dim.83
  23.5 11.0 %all-to-all-start.4 = ((bf16[32,4,2336]{2,1,0:T(4,128)(2,1)}), bf16[32,4,2336]{2,1,0:T(4,128)(2,1)S(1)}, u32[]{:S(2)}, u32[]{:S(2)}) async-start(bf16[32,4,2336]{2,1,0:T(4,128)(2,1)} %broadcast_in_dim.83), calls=%async_computation.4 | async-start | bytes 1245184 | tf_op jit(solution)/shard_map/all_to_all | solution.py:18
  34.5 1.9 convolution_convert_fusion.1
  36.5 2.5 copy.37
  39.2 21.4 %all-to-all-done.4 = bf16[32,4,2336]{2,1,0:T(4,128)(2,1)S(1)} async-done(((bf16[32,4,2336]{2,1,0:T(4,128)(2,1)}), bf16[32,4,2336]{2,1,0:T(4,128)(2,1)S(1)}, u32[]{:S(2)}, u32[]{:S(2)}) %all-to-all-start.4) | async-done | bytes 598048 | tf_op jit(solution)/shard_map/all_to_all | solution.py:18
  60.6 5.2 %all-to-all-start.1 = ((bf16[8,128,1024]{2,1,0:T(8,128)(2,1)}), bf16[8,128,1024]{2,1,0:T(8,128)(2,1)}, u32[]{:S(2)}, u32[]{:S(2)}) async-start(bf16[8,128,1024]{2,1,0:T(8,128)(2,1)} %copy.37), calls=%async_computation.1 | async-start | bytes 4194304 | tf_op jit(solution)/shard_map/all_to_all | solution.py:103
  65.8 1.1 reshape.100
  66.9 68.8 %all-gather.6.cloned.1.call-done = bf16[4194304]{0:T(1024)(128)(2,1)} async-done(((bf16[131072]{0:T(1024)(128)(2,1)}), bf16[4194304]{0:T(1024)(128)(2,1)}) %all-gather.6.cloned.1.call-update) | async-done | bytes 8388624 | tf_op jit(solution)/shard_map/all_gather | solution.py:27
  135.7 8.7 %reshape.105 = bf16[32,131072]{1,0:T(8,128)(2,1)} reshape(bf16[4194304]{0:T(1024)(128)(2,1)} %all-gather.6.cloned.1.call-done) | data formatting | bytes 16777216 | tf_op jit(solution)/shard_map/all_gather | solution.py:27
  144.4 5.8 %fusion.48 = (bf16[32,65536]{1,0:T(8,128)(2,1)}, bf16[32,65536]{1,0:T(8,128)(2,1)}) fusion(bf16[32,131072]{1,0:T(8,128)(2,1)} %reshape.105), kind=kLoop, calls=%fused_computation.57 | loop fusion | bytes 16777216 | tf_op jit(solution)/shard_map/slice | solution.py:29
  150.2 5.6 %reshape_reshape.7 = bf16[1024,2048]{1,0:T(8,128)(2,1)} reshape(bf16[32,65536]{1,0:T(8,128)(2,1)} %get-tuple-element.117) | data formatting | bytes 8388608 | tf_op jit(solution)/shard_map/reshape;reshape | solution.py:13
  155.8 5.7 %reshape_reshape.8 = bf16[2048,1024]{1,0:T(8,128)(2,1)} reshape(bf16[32,65536]{1,0:T(8,128)(2,1)} %get-tuple-element.116) | data formatting | bytes 8388608 | tf_op jit(solution)/shard_map/reshape;reshape | solution.py:13
  161.6 17.4 %while.10 = (s32[]{:T(128)}, f32[8,128,1024]{2,1,0:T(8,128)}, s32[8]{0:T(128)S(1)}, bf16[8,128,1024]{2,1,0:T(8,128)(2,1)}, f32[1,1024]{1,0:T(1,128)S(1)}, /*inde...) while((s32[]{:T(128)}, f32[8,128,1024]{2,1,0:T(8,128)}, ...), condition=%wide.region_6.7_spmd, body=%wide.region_1.6_spmd.sunk | while | flops 1077805312 | bytes 11810491 | solution.py:124
  178.9 4.1 %multiply_reduce_fusion.1 = (f32[8,128]{1,0:T(8,128)S(1)}, bf16[8,1,128,1024]{3,2,1,0:T(8,128)(2,1)S(1)}) fusion(f32[8,128,1024]{2,1,0:T(8,128)} %get-tuple-element.81, f32[1024]{0:T(1024)S(1)} %bitcast.58), kind=kLoop, calls=%fused_computation.35 | loop fusion | flops 3144704 | bytes 6299648 | tf_op jit(solution)/shard_map/reduce_sum | solution.py:125
  183.6 56.4 %all-to-all-start.5 = ((bf16[8,1,128]{2,1,0:T(2,128)(2,1)}), bf16[8,1,128]{2,1,0:T(2,128)(2,1)S(1)}, u32[]{:S(2)}, u32[]{:S(2)}) async-start(bf16[8,1,128]{2,1,0:T(2,128)(2,1)} %copy.41), calls=%async_computation.5 | async-start | bytes 8192 | tf_op jit(solution)/shard_map/all_to_all | solution.py:52
  240.0 1.6 fusion.49
  241.6 3.2 %all-to-all-done.5 = bf16[8,1,128]{2,1,0:T(2,128)(2,1)S(1)} async-done(((bf16[8,1,128]{2,1,0:T(2,128)(2,1)}), bf16[8,1,128]{2,1,0:T(2,128)(2,1)S(1)}, u32[]{:S(2)}, u32[]{:S(2)}) %all-to-all-start.5) | async-done | bytes 2080 | tf_op jit(solution)/shard_map/all_to_all | solution.py:52
  244.7 16.1 %all_to_all.38 = bf16[8,1,64,1024]{3,2,1,0:T(8,128)(2,1)S(1)} all-to-all(bf16[8,1,64,1024]{3,2,1,0:T(8,128)(2,1)} %get-tuple-element.120), channel_id=1, replica_groups=mesh['variant'=8,'mp'=32] {'variant'}, dimensions={0} | all-to-all | bytes 2097152 | tf_op jit(solution)/shard_map/all_to_all | solution.py:52
  260.8 5.9 %all-to-all-start.3 = ((bf16[8,1,64,1024]{3,2,1,0:T(8,128)(2,1)}), bf16[8,1,64,1024]{3,2,1,0:T(8,128)(2,1)S(1)}, u32[]{:S(2)}, u32[]{:S(2)}) async-start(bf16[8,1,64,1024]{3,2,1,0:T(8,128)(2,1)} %get-tuple-element.121), calls=%async_computation.3 | async-start | bytes 2097152 | tf_op jit(solution)/shard_map/all_to_all | solution.py:52
  267.5 1.5 copy.38
  269.0 7.1 %all-to-all-done.3 = bf16[8,1,64,1024]{3,2,1,0:T(8,128)(2,1)S(1)} async-done(((bf16[8,1,64,1024]{3,2,1,0:T(8,128)(2,1)}), bf16[8,1,64,1024]{3,2,1,0:T(8,128)(2,1)S(1)}, u32[]{:S(2)}, u32[]{:S(2)}) %all-to-all-start.3) | async-done | bytes 1048608 | tf_op jit(solution)/shard_map/all_to_all | solution.py:52
  276.7 2.0 fusion.40
  279.1 7.6 %fusion.36 = bf16[512,2336]{0,1:T(8,128)(2,1)} fusion(bf16[512,1024]{1,0:T(8,128)(2,1)S(1)} %bitcast.51, bf16[1024,2336]{1,0:T(8,128)(2,1)} %all-gather.4.cloned.1.call-done, pred[512]{0:T(512)(128)(4,1)S(1)} %iota_compare_fusion.1), kind=kOutput, calls=%fused_computation.36 | convolution fusion | flops 2451865600 | bytes 8225280 | tf_op jit(solution)/shard_map/dot_general | solution.py:62
  (65 shorter events, 18.5 us)
Async XLA Ops:
  7.2 27.4 %copy-start = (bf16[512,1024]{1,0:T(8,128)(2,1)S(1)}, bf16[512,1024]{1,0:T(8,128)(2,1)}, u32[]{:S(2)}) copy-start(bf16[512,1024]{1,0:T(8,128)(2,1)} %param.13) | copy-start | bytes 3145732
  7.2 128.5 %all-gather.6.cloned.1.call-start = ((), (), s32[]{:S(2)}) async-start(), calls=%async_computation.7 | async-start | bytes 8650752 | tf_op jit(solution)/shard_map/all_gather | solution.py:27
  23.5 37.1 %all-to-all-start.4 = ((bf16[32,4,2336]{2,1,0:T(4,128)(2,1)}), bf16[32,4,2336]{2,1,0:T(4,128)(2,1)S(1)}, u32[]{:S(2)}, u32[]{:S(2)}) async-start(bf16[32,4,2336]{2,1,0:T(4,128)(2,1)} %broadcast_in_dim.83), calls=%async_computation.4 | async-start | bytes 1245184 | tf_op jit(solution)/shard_map/all_to_all | solution.py:18
  60.6 100.9 %all-to-all-start.1 = ((bf16[8,128,1024]{2,1,0:T(8,128)(2,1)}), bf16[8,128,1024]{2,1,0:T(8,128)(2,1)}, u32[]{:S(2)}, u32[]{:S(2)}) async-start(bf16[8,128,1024]{2,1,0:T(8,128)(2,1)} %copy.37), calls=%async_computation.1 | async-start | bytes 4194304 | tf_op jit(solution)/shard_map/all_to_all | solution.py:103
  65.8 213.3 %all-gather.4.cloned.1.call-start = ((), (), s32[]{:S(2)}) async-start(), calls=%async_computation.6 | async-start | bytes 5603328 | tf_op jit(solution)/shard_map/all_gather | solution.py:75
  155.8 5.7 %copy-start.1 = (f32[1,1024]{1,0:T(1,128)S(1)}, f32[1,1024]{1,0:T(1,128)}, u32[]{:S(2)}) copy-start(f32[1,1024]{1,0:T(1,128)} %param.19) | copy-start | bytes 12292
  155.8 5.7 %copy-start.4 = (f32[1,1024]{1,0:T(1,128)S(1)}, f32[1,1024]{1,0:T(1,128)}, u32[]{:S(2)}) copy-start(f32[1,1024]{1,0:T(1,128)} %param.16) | copy-start | bytes 12292
  161.5 17.4 %copy-start.2 = (f32[1,1024]{1,0:T(1,128)S(1)}, f32[1,1024]{1,0:T(1,128)}, u32[]{:S(2)}) copy-start(f32[1,1024]{1,0:T(1,128)} %param.20) | copy-start | bytes 12292
  183.6 61.1 %all-to-all-start.5 = ((bf16[8,1,128]{2,1,0:T(2,128)(2,1)}), bf16[8,1,128]{2,1,0:T(2,128)(2,1)S(1)}, u32[]{:S(2)}, u32[]{:S(2)}) async-start(bf16[8,1,128]{2,1,0:T(2,128)(2,1)} %copy.41), calls=%async_computation.5 | async-start | bytes 8192 | tf_op jit(solution)/shard_map/all_to_all | solution.py:52
  240.0 26.7 %copy-start.3 = (s32[4]{0:T(128)S(1)}, s32[4]{0:T(128)}, u32[]{:S(2)}) copy-start(s32[4]{0:T(128)} %param.15) | copy-start | bytes 52
  260.8 15.3 %all-to-all-start.3 = ((bf16[8,1,64,1024]{3,2,1,0:T(8,128)(2,1)}), bf16[8,1,64,1024]{3,2,1,0:T(8,128)(2,1)S(1)}, u32[]{:S(2)}, u32[]{:S(2)}) async-start(bf16[8,1,64,1024]{3,2,1,0:T(8,128)(2,1)} %get-tuple-element.121), calls=%async_computation.3 | async-start | bytes 2097152 | tf_op jit(solution)/shard_map/all_to_all | solution.py:52
Sparse Core Ops, SparseCore 0:
  10.8 124.9 all-gather.5
  137.5 108.0 all-gather.3
where the time goes:
time: 299 us; the launch traced here: 293 us
  waiting for transfers between devices  101 us (34%)
  starting transfers between devices  78.5 us (26%)
  local copies, waits for them, and re-layouts  49.7 us (17%)
  blocking collectives  26.4 us (9%)
  between operations  14.8 us (5%)
  matrix products  11.5 us (4%)
  other arithmetic  6.58 us (2%)
  loops' own time  5.47 us (2%)
    all_gather x1, waiting for transfers between devices, one_gather(): lines, at, gathered = (lax.all_gather(ravelled, axis), 0, [])  68.8 us
    all_to_all x2, starting transfers between devices, several_exchanges(): lax.all_to_all(share, axis, split_axis=0, concat_axis=0, tiled=True)  62.2 us
    all_to_all x1, waiting for transfers between devices, from_everyone(): lax.all_to_all(jnp.broadcast_to(x[None], (size, *x.shape)), axis, 0, 0, t...  21.4 us
    all_to_all x1, blocking collectives, several_exchanges(): lax.all_to_all(share, axis, split_axis=0, concat_axis=0, tiled=True)  16.1 us
    another operation x2, local copies, waits for them, and re-layouts, laid_out(): parts.reshape(*shape[:dim], shape[dim] * shape[dim + 1], *shape[dim + 2:])  11.3 us
    all_to_all x1, starting transfers between devices, from_everyone(): lax.all_to_all(jnp.broadcast_to(x[None], (size, *x.shape)), axis, 0, 0, t...  11 us
    all_to_all x1, blocking collectives, local(): lax.all_to_all(out_live, 'variant', split_axis=0, concat_axis=0, tiled=True)  10.4 us
    all_to_all x2, waiting for transfers between devices, several_exchanges(): lax.all_to_all(share, axis, split_axis=0, concat_axis=0, tiled=True)  10.3 us
  transfers between devices with their start and end apart: 6, of which 4 were waited for; matrix products, arithmetic and copies ran while one was open for 20% of the time, Pallas kernels for 0%

commit v1 on v0

v1 whole, which is shorter than its diff:
```python
import functools

import jax
import jax.numpy as jnp
from jax import lax
from jax.experimental import pallas as pl
from jax.experimental.pallas import tpu as pltpu
from jax.sharding import PartitionSpec as P

MESH = pl.DeviceIdType.MESH
BLOCK = 128
EPS = 1e-06
XLO, XHI, CORES = 2, 2, 2
GROUP = 2


def rms_scale(values, gain):
    mean_square = jnp.mean(values * values, axis=-1, keepdims=True)
    return values * lax.rsqrt(mean_square + EPS) * gain


def remote(src, dst, send_sem, recv_sem, device):
    return pltpu.make_async_remote_copy(
        src_ref=src, dst_ref=dst, send_sem=send_sem, recv_sem=recv_sem, device_id=device, device_id_type=MESH
    )


def exchange_kernel(
    variants,
    members,
    bv_ref,
    pos_ref,
    up_ref,
    down_ref,
    ng_ref,
    fg_ref,
    vw_ref,
    hid_out,
    val_out,
    outgoing,
    incoming,
    normed,
    active,
    up_all,
    down_all,
    hidden,
    returned,
    estimate,
    estimate_back,
    ring_recv,
    plus_send,
    minus_send,
    core_send,
    half_send,
    slot_send,
    slot_recv,
    back_send,
    back_recv,
    value_send,
    value_recv,
):
    ys, zs = variants // XLO, members // (XHI * CORES)
    v, m = lax.axis_index("variant"), lax.axis_index("mp")
    y, xl = lax.div(v, XLO), lax.rem(v, XLO)
    xh, z, core = lax.div(m, zs * CORES), lax.rem(lax.div(m, CORES), zs), lax.rem(m, CORES)

    def member(xr, dz, cr):
        return (lax.rem(xh + xr, XHI) * zs + lax.rem(z + dz, zs)) * CORES + lax.rem(core + cr, CORES)

    def peer(dy, dx):
        return lax.rem(y + dy, ys) * XLO + lax.rem(xl + dx, XLO)

    z_plus, z_minus = (v, member(0, 1, 0)), (v, member(0, zs - 1, 0))
    sibling, half = (v, member(0, 0, 1)), (v, member(1, 0, 0))
    order = sorted(
        ((dy, dx) for dy in range(ys) for dx in range(XLO)), key=lambda r: (-min(r[0], ys - r[0]), -r[1])
    )
    to_peer = [(peer(dy, dx), m) for dy, dx in order]
    from_peer = [(peer(ys - dy, XLO - dx), m) for dy, dx in order]
    slots = len(order)
    local = slots - 1

    barrier = pltpu.get_barrier_semaphore()
    greeted = [z_plus, z_minus, sibling, half, *to_peer[:local]]
    for device in greeted:
        pl.semaphore_signal(barrier, inc=1, device_id=device, device_id_type=MESH)
    pl.semaphore_wait(barrier, len(greeted))

    shards, wholes = (up_ref, down_ref), (up_all, down_all)

    def rows(kind, xr, dist, cr):
        depth = shards[kind].shape[0]
        owner = member(xr, zs - dist, cr)
        return wholes[kind].at[pl.ds(pl.multiple_of(owner * depth, depth), depth)]

    def source(kind, xr, dist):
        return shards[kind] if (xr, dist) == (0, 0) else rows(kind, xr, dist, 0)

    sent = []

    def send(copy):
        copy.start()
        sent.append(copy)

    def send_half(kind):
        send(remote(shards[kind], rows(kind, 0, 0, 0), half_send.at[kind], ring_recv.at[kind, 1, 0, 0], half))

    def send_plus(kind, xr, dist):
        send(
            remote(
                source(kind, xr, dist),
                rows(kind, xr, dist, 0),
                plus_send.at[kind, xr, dist],
                ring_recv.at[kind, xr, dist + 1, 0],
                z_plus,
            )
        )

    def send_minus(kind, xr, dist):
        send(
            remote(
                source(kind, xr, dist),
                rows(kind, xr, dist, 0),
                minus_send.at[kind, xr, dist],
                ring_recv.at[kind, xr, (dist - 1) % zs, 0],
                z_minus,
            )
        )

    def send_core(kind, xr, dist):
        send(
            remote(
                source(kind, xr, dist),
                rows(kind, xr, dist, 0),
                core_send.at[kind, xr, dist],
                ring_recv.at[kind, xr, dist, 1],
                sibling,
            )
        )

    def arrived(kind, xr, dist, cr):
        ref = rows(kind, xr, dist, cr)
        remote(ref, ref, core_send.at[kind, xr, dist], ring_recv.at[kind, xr, dist, cr], sibling).wait_recv()

    plus = (zs // 2, zs - 1 - zs // 2)
    minus = (zs - 1 - zs // 2, zs // 2)
    steps = zs // 2

    def begin_own(kind):
        send_plus(kind, 0, 0)
        send_minus(kind, 0, 0)
        send_core(kind, 0, 0)

    def begin_half(kind):
        arrived(kind, 1, 0, 0)
        send_plus(kind, 1, 0)
        send_minus(kind, 1, 0)
        send_core(kind, 1, 0)

    def ring_step(kind, step):
        for xr in range(XHI):
            if step <= plus[kind]:
                arrived(kind, xr, step, 0)
                if step < plus[kind]:
                    send_plus(kind, xr, step)
                send_core(kind, xr, step)
            if step <= minus[kind]:
                arrived(kind, xr, zs - step, 0)
                if step < minus[kind]:
                    send_minus(kind, xr, zs - step)
                send_core(kind, xr, zs - step)

    send_half(0)
    begin_own(0)
    send_half(1)

    def fill(k):
        wanted = to_peer[k][0]
        block = pos_ref[0:BLOCK, :]
        for b in range(1, bv_ref.shape[0]):
            block = jnp.where(bv_ref[b] == wanted, pos_ref[b * BLOCK : (b + 1) * BLOCK, :], block)
        if k == local:
            incoming[k] = block
        else:
            outgoing[k] = block

    def dispatch(k):
        send(remote(outgoing.at[k], incoming.at[k], slot_send.at[k], slot_recv.at[k], to_peer[k]))

    fill(0)
    for k in range(1, slots):
        fill(k)
        dispatch(k - 1)

    for kind in range(2):
        depth = shards[kind].shape[0]
        wholes[kind][pl.ds(pl.multiple_of(m * depth, depth), depth), :] = shards[kind][...]

    begin_half(0)
    for step in range(1, steps):
        ring_step(0, step)
    begin_own(1)
    begin_half(1)
    ring_step(0, steps)
    for step in range(1, steps):
        ring_step(1, step)

    for k in range(slots):
        if k != local:
            remote(outgoing.at[k], incoming.at[k], slot_send.at[k], slot_recv.at[k], to_peer[k]).wait_recv()
        normed[pl.ds(k * BLOCK, BLOCK), :] = rms_scale(incoming[k].astype(jnp.float32), ng_ref[...]).astype(
            jnp.bfloat16
        )
    for xr in range(XHI):
        for dist in range(zs):
            arrived(0, xr, dist, 1)

    total_rows = normed.shape[0]
    part_rows = total_rows // 2
    width = 256
    tiles = up_all.shape[1] // width

    def up_tiles(first, last):
        def one(i, carry):
            col = pl.multiple_of(lax.div(i, 2) * width, width)
            row = pl.multiple_of(lax.rem(i, 2) * part_rows, part_rows)
            upward = jnp.dot(
                normed[pl.ds(row, part_rows), :],
                up_all[:, pl.ds(col, width)],
                preferred_element_type=jnp.float32,
            )
            active[pl.ds(row, part_rows), pl.ds(col, width)] = jax.nn.gelu(upward, approximate=True).astype(
                jnp.bfloat16
            )
            return carry

        lax.fori_loop(2 * first, 2 * last, one, 0)

    up_tiles(0, tiles // 2)
    ring_step(1, steps)
    up_tiles(tiles // 2, tiles)
    for xr in range(XHI):
        for dist in range(zs):
            arrived(1, xr, dist, 1)

    def give_back(k):
        send(remote(hidden.at[k], returned.at[k], back_send.at[k], back_recv.at[k], from_peer[k]))
        send(remote(estimate.at[k], estimate_back.at[k], value_send.at[k], value_recv.at[k], from_peer[k]))

    for first in range(0, slots, GROUP):
        downward = jnp.dot(
            active[pl.ds(first * BLOCK, GROUP * BLOCK), :], down_all[...], preferred_element_type=jnp.float32
        )
        for k in range(first, first + GROUP):
            part = downward[(k - first) * BLOCK : (k - first + 1) * BLOCK]
            final = rms_scale(incoming[k].astype(jnp.float32) + part, fg_ref[...])
            kept, kept_value = (returned, estimate_back) if k == local else (hidden, estimate)
            kept[k] = final.astype(jnp.bfloat16)
            value = jnp.tanh(jnp.sum(final * vw_ref[...], axis=-1, keepdims=True))
            kept_value[k] = jnp.transpose(jnp.broadcast_to(value, (BLOCK, BLOCK)))[0:8]
        for k in range(first, first + GROUP):
            if k != local:
                give_back(k)

    for k in range(slots):
        if k != local:
            remote(hidden.at[k], returned.at[k], back_send.at[k], back_recv.at[k], from_peer[k]).wait_recv()
            remote(
                estimate.at[k], estimate_back.at[k], value_send.at[k], value_recv.at[k], from_peer[k]
            ).wait_recv()

    for b in range(bv_ref.shape[0]):
        block, value = returned[0], estimate_back[0]
        for k in range(1, slots):
            chosen = bv_ref[b] == to_peer[k][0]
            block = jnp.where(chosen, returned[k], block)
            value = jnp.where(chosen, estimate_back[k], value)
        hid_out[pl.ds(b * BLOCK, BLOCK), :] = block
        val_out[pl.ds(b, 1), :] = value[0:1]

    for copy in sent:
        copy.wait_send()


def local(
    positions,
    game_counts,
    block_variant,
    norm_gain,
    up_weight,
    down_weight,
    final_gain,
    value_weight,
    policy_weight,
):
    variants, members = lax.axis_size("variant"), lax.axis_size("mp")
    zs = members // (XHI * CORES)
    games_here, width = positions.shape
    blocks = block_variant.shape[0]
    up_rows, ffw = up_weight.shape[1:]
    down_rows = down_weight.shape[1]
    slots = variants
    vmem = pl.BlockSpec(memory_space=pltpu.VMEM)
    dma = pltpu.SemaphoreType.DMA
    policy_whole = lax.all_gather(policy_weight, ("variant", "mp"), axis=0, tiled=True)
    own_hidden, own_value = pl.pallas_call(
        functools.partial(exchange_kernel, variants, members),
        out_shape=(
            jax.ShapeDtypeStruct((games_here, width), jnp.bfloat16),
            jax.ShapeDtypeStruct((blocks, BLOCK), jnp.float32),
        ),
        in_specs=[pl.BlockSpec(memory_space=pltpu.SMEM)] + [vmem] * 6,
        out_specs=(vmem, vmem),
        scratch_shapes=[
            pltpu.VMEM((slots, BLOCK, width), jnp.bfloat16),
            pltpu.VMEM((slots, BLOCK, width), jnp.bfloat16),
            pltpu.VMEM((slots * BLOCK, width), jnp.bfloat16),
            pltpu.VMEM((slots * BLOCK, ffw), jnp.bfloat16),
            pltpu.VMEM((up_rows * members, ffw), jnp.bfloat16),
            pltpu.VMEM((down_rows * members, width), jnp.bfloat16),
            pltpu.VMEM((slots, BLOCK, width), jnp.bfloat16),
            pltpu.VMEM((slots, BLOCK, width), jnp.bfloat16),
            pltpu.VMEM((slots, 8, BLOCK), jnp.float32),
            pltpu.VMEM((slots, 8, BLOCK), jnp.float32),
            dma((2, XHI, zs, CORES)),
            dma((2, XHI, zs)),
            dma((2, XHI, zs)),
            dma((2, XHI, zs)),
            dma((2,)),
            dma((slots,)),
            dma((slots,)),
            dma((slots,)),
            dma((slots,)),
            dma((slots,)),
            dma((slots,)),
        ],
        compiler_params=pltpu.CompilerParams(
            collective_id=0, has_side_effects=True, vmem_limit_bytes=52 * 1024 * 1024
        ),
        cost_estimate=pl.CostEstimate(
            flops=4 * slots * BLOCK * width * ffw, bytes_accessed=4 * width * ffw, transcendentals=0
        ),
        name="exchange",
    )(block_variant, positions, up_weight[0], down_weight[0], norm_gain, final_gain, value_weight)
    logits = jnp.dot(own_hidden, policy_whole, preferred_element_type=jnp.float32).astype(jnp.bfloat16)
    row_live = jnp.arange(games_here, dtype=jnp.int32) < game_counts[0]
    policy = jnp.where(row_live[:, None], logits, jnp.zeros((), jnp.bfloat16))
    value = jnp.where(row_live, own_value.reshape(games_here), jnp.zeros((), jnp.float32))
    return (policy, value)


def solution(mesh):
    in_specs = (
        P(("variant", "mp"), None),
        P(("variant", "mp")),
        P(("variant", "mp")),
        P("variant", None),
        P("variant", "mp", None),
        P("variant", "mp", None),
        P("variant", None),
        P("variant", None),
        P(("variant", "mp"), None),
    )
    out_specs = (P(("variant", "mp"), None), P(("variant", "mp")))
    return jax.shard_map(local, mesh=mesh, in_specs=in_specs, out_specs=out_specs, check_vma=False)
```

time: 299 us -> 472 us (1.58)
  waiting for transfers between devices: 101 us -> 340 us
  Pallas kernels: 0 us -> 91.1 us
  starting transfers between devices: 78.5 us -> 0.04 us
  local copies, waits for them, and re-layouts: 49.7 us -> 13.2 us
  blocking collectives: 26.4 us -> 0 us
  other arithmetic: 6.58 us -> 0.59 us
  loops' own time: 5.47 us -> 0 us
    all_gather x2 -> x1, waiting for transfers between devices: 68.8 us -> 340 us  [local(): lax.all_gather(policy_weight, ('variant', 'mp'), axis=0, tiled=True)]
    pallas_call x0 -> x1, Pallas kernels: none -> 91.1 us  [local(): pl.pallas_call(functools.partial(exchange_kernel, variants, members), out...]
    all_to_all x4 -> x0, starting transfers between devices: 78.4 us -> none  [the longest x2 62.2 us: several_exchanges(): lax.all_to_all(share, axis, split_axis=0, concat_axis=0, tiled=True)]
    all_to_all x4 -> x0, waiting for transfers between devices: 31.7 us -> none  [the longest x1 21.4 us: from_everyone(): lax.all_to_all(jnp.broadcast_to(x[None], (size, *x.shape)), axis, 0, 0, t...]
    all_to_all x2 -> x0, blocking collectives: 26.4 us -> none  [the longest x1 16.1 us: several_exchanges(): lax.all_to_all(share, axis, split_axis=0, concat_axis=0, tiled=True)]
    another operation x2 -> x0, local copies, waits for them, and re-layouts: 11.3 us -> none  [laid_out(): parts.reshape(*shape[:dim], shape[dim] * shape[dim + 1], *shape[dim + 2:])]
    unnamed x12 -> x13, local copies, waits for them, and re-layouts: 1.96 us -> 13.2 us
    all_gather x1 -> x0, local copies, waits for them, and re-layouts: 8.66 us -> none  [one_gather(): lines, at, gathered = (lax.all_gather(ravelled, axis), 0, [])]
  transfers between devices with their start and end apart: 6 -> 1, of which waited for: 4 -> 1; matrix products, arithmetic and copies ran while one was open for 20% -> 0% of each run, Pallas kernels for 0% -> 19%
where the time goes in v1:
time: 472 us; the launch traced here: 468 us
  waiting for transfers between devices  340 us (72%)
  Pallas kernels  91.1 us (19%)
  between operations  14.7 us (3%)
  local copies, waits for them, and re-layouts  13.2 us (3%)
  matrix products  7.55 us (2%)
    all_gather x1, waiting for transfers between devices, local(): lax.all_gather(policy_weight, ('variant', 'mp'), axis=0, tiled=True)  340 us
    pallas_call x1, Pallas kernels, local(): pl.pallas_call(functools.partial(exchange_kernel, variants, members), out...  91.1 us
    unnamed x13, local copies, waits for them, and re-layouts  13.2 us
  transfers between devices with their start and end apart: 1, of which 1 were waited for; matrix products, arithmetic and copies ran while one was open for 0% of the time, Pallas kernels for 19%

profile of v1, /device:TPU:8, one launch (start us, length us, event | category | flops | bytes accessed | tf_op | source)
XLA Modules:
  0.0 467.6 jit_solution(6415976099046964252)
XLA Ops:
  7.2 0.0 all-gather.3.cloned.1.call-start
  7.2 0.7 all-gather.3.cloned.1.call-update
  8.6 0.0 copy-start
  8.6 0.9 copy-done
  9.5 0.0 copy-start.1
  9.5 0.9 copy-done.1
  10.4 0.0 copy-start.2
  10.4 0.7 copy-done.2
  11.1 0.0 copy-start.3
  11.1 0.7 copy-done.3
  11.7 0.0 copy-start.4
  11.7 0.7 copy-done.4
  12.4 0.0 copy-start.5
  12.4 0.7 copy-done.5
  13.1 91.1 %exchange.1 = (bf16[512,1024]{1,0:T(8,128)(2,1)S(1)}, f32[4,128]{1,0:T(4,128)S(1)}) custom-call(s32[4]{0:T(128)S(1)} %copy-done.5, bf16[512,1024]{1,0:T(8,128)(2,1)} %pos_ref.1, bf16[32,2048]{1,0:T(8,128)(2,1)S(1)} %bitcast.10, bf16[64,1024]{1,0:T(8,128)(2,1)S(1)} %bitcast.11, f32[1,1024]{1,0:T(1,128)S(1)} %copy-done.2, f32[1,1024]{1,0:T(1,128)S(1)} %copy-done.3, ...), custom_call_target="tpu_custom_call" | custom-call | flops 8589934592 | bytes 8388608 | tf_op jit(solution)/shard_map/exchange/pallas_call | solution.py:306
  104.2 0.6 bitcast_select_fusion
  104.7 339.8 %all-gather.3.cloned.1.call-done = bf16[256,4,2336]{2,1,0:T(4,128)(2,1)} async-done(((bf16[1,4,2336]{2,1,0:T(4,128)(2,1)}), bf16[256,4,2336]{2,1,0:T(4,128)(2,1)}) %all-gather.3.cloned.1.call-update) | async-done | bytes 4784144 | tf_op jit(solution)/shard_map/all_gather | solution.py:305
  444.5 8.7 %reshape.13 = bf16[1024,2336]{1,0:T(8,128)(2,1)} reshape(bf16[256,4,2336]{2,1,0:T(4,128)(2,1)} %all-gather.3.cloned.1.call-done) | data formatting | bytes 9568256
  453.2 7.5 %fusion = bf16[512,2336]{0,1:T(8,128)(2,1)} fusion(bf16[512,1024]{1,0:T(8,128)(2,1)S(1)} %get-tuple-element.4, bf16[1024,2336]{1,0:T(8,128)(2,1)} %reshape.13, pred[512]{0:T(512)(128)(4,1)S(1)} %iota_compare_fusion), kind=kOutput, calls=%fused_computation.1 | convolution fusion | flops 2451865600 | bytes 8225280 | tf_op jit(solution)/shard_map/dot_general | solution.py:345
  (1 shorter events, 0.0 us)
Async XLA Ops:
  7.2 437.4 %all-gather.3.cloned.1.call-start = ((), (), s32[]{:S(2)}) async-start(), calls=%async_computation | async-start | bytes 5000192 | tf_op jit(solution)/shard_map/all_gather | solution.py:305
  8.6 0.9 copy-start
  9.5 0.9 copy-start.1
  10.4 0.7 copy-start.2
  11.1 0.7 copy-start.3
  11.7 0.7 copy-start.4
  12.4 0.7 copy-start.5
Sparse Core Ops, SparseCore 0:
  9.9 434.6 all-gather.2

commit v2 on v1

--- a/solution.py
+++ b/solution.py
@@ -35,7 +35,9 @@
     ng_ref,
     fg_ref,
     vw_ref,
-    hid_out,
+    count_ref,
+    piece_ref,
+    policy_out,
     val_out,
     outgoing,
     incoming,
@@ -58,6 +60,19 @@
     back_recv,
     value_send,
     value_recv,
+    own_hidden,
+    policy_all,
+    pieces,
+    piece_send,
+    piece_recv,
+    pair_send,
+    pair_recv,
+    first_send,
+    first_recv,
+    second_send,
+    second_recv,
+    policy_core_send,
+    policy_core_recv,
 ):
     ys, zs = variants // XLO, members // (XHI * CORES)
     v, m = lax.axis_index("variant"), lax.axis_index("mp")
@@ -80,8 +95,42 @@
     slots = len(order)
     local = slots - 1
 
+    half_columns = policy_all.shape[1] // CORES
+    tile_rows = piece_ref.shape[0]
+    unit_rows = zs // 2 * tile_rows
+    paired = z + 1 - 2 * lax.rem(z, 2) - z
+    other_z = (v, member(0, zs + paired, 0))
+    other_z_sibling = (v, member(0, zs + paired, 1))
+    x = xh * XLO + xl
+    xs = XHI * XLO
+
+    def chip(cx, cy):
+        cx, cy = lax.rem(cx, xs), lax.rem(cy, ys)
+        return cy * XLO + lax.rem(cx, XLO), (lax.div(cx, XLO) * zs + z) * CORES + core
+
+    def along(first, second):
+        return x + first * (1 - core) + second * core, y + first * core + second * (1 - core)
+
+    first_plus, first_minus = chip(*along(1, 0)), chip(*along(3, 0))
+    second_plus, second_minus = chip(*along(0, 1)), chip(*along(0, 3))
+    skips = (2, zs - 2, zs // 2)
+    skip_to = [(v, member(0, d, 0)) for d in skips]
+
+    def policy_rows(a, b, cr, start=0, count=None):
+        axis = lax.rem(core + cr, CORES)
+        cx = lax.rem(x + (xs - a) * (1 - axis) + (xs - b) * axis, xs)
+        cy = lax.rem(y + (ys - a) * axis + (ys - b) * (1 - axis), ys)
+        group = (cy * XLO + lax.rem(cx, XLO)) * XHI + lax.div(cx, XLO)
+        row = pl.multiple_of(group * unit_rows + start, tile_rows)
+        column = pl.multiple_of(axis * half_columns, 128)
+        return policy_all.at[pl.ds(row, unit_rows if count is None else count), pl.ds(column, half_columns)]
+
+    def policy_tile(dz):
+        return policy_rows(0, 0, 0, lax.div(lax.rem(z + dz, zs), 2) * tile_rows, tile_rows)
+
     barrier = pltpu.get_barrier_semaphore()
     greeted = [z_plus, z_minus, sibling, half, *to_peer[:local]]
+    greeted += [other_z_sibling, (peer(0, 1), member(1, 0, 0)), *skip_to]
     for device in greeted:
         pl.semaphore_signal(barrier, inc=1, device_id=device, device_id_type=MESH)
     pl.semaphore_wait(barrier, len(greeted))
@@ -170,6 +219,80 @@
                     send_minus(kind, xr, zs - step)
                 send_core(kind, xr, zs - step)
 
+    own_columns = pl.ds(pl.multiple_of(core * half_columns, 128), half_columns)
+    sibling_columns = pl.ds(pl.multiple_of((1 - core) * half_columns, 128), half_columns)
+
+    def piece_copy(i):
+        columns = own_columns if i == 1 else sibling_columns
+        device = (sibling, other_z, other_z_sibling)[i]
+        return remote(piece_ref.at[:, columns], pieces.at[i], piece_send.at[i], piece_recv.at[i], device)
+
+    def merge_pieces():
+        total = piece_ref[:, own_columns].astype(jnp.float32)
+        for i in range(3):
+            piece_copy(i).wait_recv()
+            total = total + pieces[i].astype(jnp.float32)
+        policy_tile(0)[...] = total.astype(jnp.bfloat16)
+
+    def skip_copy(i, dz):
+        ref = policy_tile(dz)
+        return remote(ref, ref, pair_send.at[i], pair_recv.at[i], skip_to[i])
+
+    def send_skips():
+        for i in range(len(skips)):
+            send(skip_copy(i, 0))
+
+    def policy_to_core(a, b):
+        ref = policy_rows(a, b, 0)
+        send(remote(ref, ref, policy_core_send.at[a, b], policy_core_recv.at[a, b], sibling))
+
+    part_unit = unit_rows // 2
+
+    def first_copy(i, a):
+        ref = policy_rows(a, 0, 0) if i < 2 else policy_rows(a, 0, 0, (i - 2) * part_unit, part_unit)
+        return remote(ref, ref, first_send.at[i], first_recv.at[i], (first_plus, first_minus)[i % 2])
+
+    def first_begin():
+        for i, dz in enumerate(skips):
+            skip_copy(i, zs - dz).wait_recv()
+        send(first_copy(0, 0))
+        send(first_copy(1, 0))
+        policy_to_core(0, 0)
+
+    def first_forward():
+        for i, a in ((0, 1), (1, 3)):
+            first_copy(i, a).wait_recv()
+            send(first_copy(2 + i, a))
+            policy_to_core(a, 0)
+
+    def second_copy(a, i, b):
+        ref = policy_rows(a, b, 0)
+        device = second_plus if i == 0 or (i == 2 and a < 2) else second_minus
+        return remote(ref, ref, second_send.at[a, i], second_recv.at[a, i], device)
+
+    def second_begin():
+        for i in (2, 3):
+            first_copy(i, 2).wait_recv()
+        policy_to_core(2, 0)
+        for a in range(xs):
+            send(second_copy(a, 0, 0))
+            send(second_copy(a, 1, 0))
+
+    def second_forward():
+        for a in range(xs):
+            for i, b in ((0, 1), (1, 3)):
+                second_copy(a, i, b).wait_recv()
+                if (i == 0) == (a < 2):
+                    send(second_copy(a, 2, b))
+                policy_to_core(a, b)
+
+    def second_end():
+        for a in range(xs):
+            second_copy(a, 2, 2).wait_recv()
+            policy_to_core(a, 2)
+
+    for i in range(3):
+        send(piece_copy(i))
     send_half(0)
     begin_own(0)
     send_half(1)
@@ -187,22 +310,32 @@
     def dispatch(k):
         send(remote(outgoing.at[k], incoming.at[k], slot_send.at[k], slot_recv.at[k], to_peer[k]))
 
-    fill(0)
-    for k in range(1, slots):
+    for k in range(slots):
         fill(k)
-        dispatch(k - 1)
+    dispatch(0)
+    dispatch(1)
 
     for kind in range(2):
         depth = shards[kind].shape[0]
         wholes[kind][pl.ds(pl.multiple_of(m * depth, depth), depth), :] = shards[kind][...]
 
+    merge_pieces()
     begin_half(0)
-    for step in range(1, steps):
+    ring_step(0, 1)
+    send_skips()
+    ring_step(0, 2)
+    first_begin()
+    for k in range(2, local):
+        dispatch(k)
+    for step in range(3, steps):
         ring_step(0, step)
     begin_own(1)
     begin_half(1)
     ring_step(0, steps)
-    for step in range(1, steps):
+    first_forward()
+    ring_step(1, 1)
+    second_begin()
+    for step in range(2, steps):
         ring_step(1, step)
 
     for k in range(slots):
@@ -238,6 +371,7 @@
 
     up_tiles(0, tiles // 2)
     ring_step(1, steps)
+    second_forward()
     up_tiles(tiles // 2, tiles)
     for xr in range(XHI):
         for dist in range(zs):
@@ -262,21 +396,47 @@
             if k != local:
                 give_back(k)
 
+    second_end()
     for k in range(slots):
         if k != local:
             remote(hidden.at[k], returned.at[k], back_send.at[k], back_recv.at[k], from_peer[k]).wait_recv()
             remote(
                 estimate.at[k], estimate_back.at[k], value_send.at[k], value_recv.at[k], from_peer[k]
             ).wait_recv()
-
+    for a in range(xs):
+        for b in range(ys):
+            ref = policy_rows(a, b, 1)
+            remote(ref, ref, policy_core_send.at[a, b], policy_core_recv.at[a, b], sibling).wait_recv()
+
+    count = count_ref[0]
     for b in range(bv_ref.shape[0]):
         block, value = returned[0], estimate_back[0]
         for k in range(1, slots):
             chosen = bv_ref[b] == to_peer[k][0]
             block = jnp.where(chosen, returned[k], block)
             value = jnp.where(chosen, estimate_back[k], value)
-        hid_out[pl.ds(b * BLOCK, BLOCK), :] = block
-        val_out[pl.ds(b, 1), :] = value[0:1]
+        own_hidden[pl.ds(b * BLOCK, BLOCK), :] = block
+        games = b * BLOCK + lax.broadcasted_iota(jnp.int32, (1, BLOCK), 1)
+        val_out[pl.ds(b, 1), :] = jnp.where(games < count, value[0:1], 0.0)
+
+    games_here, moves = policy_out.shape
+    live = lax.broadcasted_iota(jnp.int32, (games_here, 1), 0) < count
+
+    def masked_logits(columns):
+        logits = jnp.dot(own_hidden[...], policy_all[:, columns], preferred_element_type=jnp.float32)
+        return jnp.where(live, logits, 0.0).astype(jnp.bfloat16)
+
+    whole_tiles = moves // width
+
+    def policy_tile_step(i, carry):
+        columns = pl.ds(pl.multiple_of(i * width, width), width)
+        policy_out[:, columns] = masked_logits(columns)
+        return carry
+
+    lax.fori_loop(0, whole_tiles, policy_tile_step, 0)
+    rest = moves - whole_tiles * width
+    if rest:
+        policy_out[:, pl.ds(whole_tiles * width, rest)] = masked_logits(pl.ds(whole_tiles * width, width))[:, :rest]
 
     for copy in sent:
         copy.wait_send()
@@ -302,14 +462,22 @@
     slots = variants
     vmem = pl.BlockSpec(memory_space=pltpu.VMEM)
     dma = pltpu.SemaphoreType.DMA
-    policy_whole = lax.all_gather(policy_weight, ("variant", "mp"), axis=0, tiled=True)
-    own_hidden, own_value = pl.pallas_call(
+    policy_rows_here, moves = policy_weight.shape
+    half_columns = -(-moves // (CORES * 128)) * 128
+    tile_rows = 2 * CORES * policy_rows_here
+    widened = jnp.pad(policy_weight, ((0, 0), (0, CORES * half_columns - moves)))
+    place = lax.rem(lax.axis_index("mp"), 2 * CORES)
+    in_place = lax.div(jnp.arange(tile_rows, dtype=jnp.int32), policy_rows_here) == place
+    piece = jnp.where(in_place[:, None], jnp.tile(widened, (2 * CORES, 1)), jnp.zeros((), jnp.bfloat16))
+    policy, value = pl.pallas_call(
         functools.partial(exchange_kernel, variants, members),
         out_shape=(
-            jax.ShapeDtypeStruct((games_here, width), jnp.bfloat16),
+            jax.ShapeDtypeStruct((games_here, moves), jnp.bfloat16),
             jax.ShapeDtypeStruct((blocks, BLOCK), jnp.float32),
         ),
-        in_specs=[pl.BlockSpec(memory_space=pltpu.SMEM)] + [vmem] * 6,
+        in_specs=[pl.BlockSpec(memory_space=pltpu.SMEM)]
+        + [vmem] * 6
+        + [pl.BlockSpec(memory_space=pltpu.SMEM), vmem],
         out_specs=(vmem, vmem),
         scratch_shapes=[
             pltpu.VMEM((slots, BLOCK, width), jnp.bfloat16),
@@ -333,20 +501,39 @@
             dma((slots,)),
             dma((slots,)),
             dma((slots,)),
+            pltpu.VMEM((games_here, width), jnp.bfloat16),
+            pltpu.VMEM((variants * members * policy_rows_here, CORES * half_columns), jnp.bfloat16),
+            pltpu.VMEM((3, tile_rows, half_columns), jnp.bfloat16),
+            dma((3,)),
+            dma((3,)),
+            dma((3,)),
+            dma((3,)),
+            dma((4,)),
+            dma((4,)),
+            dma((4, 3)),
+            dma((4, 3)),
+            dma((4, 4)),
+            dma((4, 4)),
         ],
         compiler_params=pltpu.CompilerParams(
-            collective_id=0, has_side_effects=True, vmem_limit_bytes=52 * 1024 * 1024
+            collective_id=0, has_side_effects=True, vmem_limit_bytes=58 * 1024 * 1024
         ),
         cost_estimate=pl.CostEstimate(
             flops=4 * slots * BLOCK * width * ffw, bytes_accessed=4 * width * ffw, transcendentals=0
         ),
         name="exchange",
-    )(block_variant, positions, up_weight[0], down_weight[0], norm_gain, final_gain, value_weight)
-    logits = jnp.dot(own_hidden, policy_whole, preferred_element_type=jnp.float32).astype(jnp.bfloat16)
-    row_live = jnp.arange(games_here, dtype=jnp.int32) < game_counts[0]
-    policy = jnp.where(row_live[:, None], logits, jnp.zeros((), jnp.bfloat16))
-    value = jnp.where(row_live, own_value.reshape(games_here), jnp.zeros((), jnp.float32))
-    return (policy, value)
+    )(
+        block_variant,
+        positions,
+        up_weight[0],
+        down_weight[0],
+        norm_gain,
+        final_gain,
+        value_weight,
+        game_counts,
+        piece,
+    )
+    return (policy, value.reshape(games_here))
 
 
 def solution(mesh):

time: 472 us -> 112 us (0.24)
  waiting for transfers between devices: 340 us -> 0 us
  between operations: 14.7 us -> 1.32 us
  Pallas kernels: 91.1 us -> 102 us
  matrix products: 7.55 us -> 0 us
  local copies, waits for them, and re-layouts: 13.2 us -> 5.69 us
    all_gather x1 -> x0, waiting for transfers between devices: 340 us -> none  [local(): lax.all_gather(policy_weight, ('variant', 'mp'), axis=0, tiled=True)]
    pallas_call x1, Pallas kernels: 91.1 us -> 102 us  [local(): pl.pallas_call(functools.partial(exchange_kernel, variants, members), out...]
    unnamed x13 -> x4, local copies, waits for them, and re-layouts: 13.2 us -> 4.9 us
    dot_general x1 -> x0, matrix products: 7.55 us -> none  [local(): jnp.dot(own_hidden, policy_whole, preferred_element_type=jnp.float32)]
  transfers between devices with their start and end apart: 1 -> 0, of which waited for: 1 -> 0; matrix products, arithmetic and copies ran while one was open for 0% -> 0% of each run, Pallas kernels for 19% -> 0%
where the time goes in v2:
time: 112 us; the launch traced here: 110 us
  Pallas kernels  102 us (91%)
  local copies, waits for them, and re-layouts  5.69 us (5%)
  between operations  1.32 us (1%)
    pallas_call x1, Pallas kernels, local(): pl.pallas_call(functools.partial(exchange_kernel, variants, members), out...  102 us
    unnamed x4, local copies, waits for them, and re-layouts  4.9 us

profile of v2, /device:TPU:8, one launch (start us, length us, event | category | flops | bytes accessed | tf_op | source)
XLA Modules:
  0.0 109.7 jit_solution(16381551962322280173)
XLA Ops:
  1.3 0.7 pad.4
  2.1 0.7 broadcast_select_fusion.piece_ref
  2.8 102.0 %exchange.1 = (bf16[512,2336]{1,0:T(8,128)(2,1)}, f32[4,128]{1,0:T(4,128)}) custom-call(s32[4]{0:T(128)} %bv_ref.1, bf16[512,1024]{1,0:T(8,128)(2,1)} %pos_ref.1, bf16[32,2048]{1,0:T(8,128)(2,1)} %bitcast.4, bf16[64,1024]{1,0:T(8,128)(2,1)} %bitcast.5, f32[1,1024]{1,0:T(1,128)} %ng_ref.1, f32[1,1024]{1,0:T(1,128)} %fg_ref.1, f32[1,1024]{1,0:T(1,128)} %vw_ref.1, ...), custom_call_target="tpu_custom_call" | custom-call | flops 8589934592 | bytes 8388608 | tf_op jit(solution)/shard_map/exchange/pallas_call | solution.py:472
  104.8 0.0 copy-start
  104.8 4.3 %copy.11 = bf16[512,2336]{0,1:T(8,128)(2,1)} copy(bf16[512,2336]{1,0:T(8,128)(2,1)} %get-tuple-element.6) | data formatting | bytes 4784128
  109.1 0.0 copy-done
  109.1 0.6 copy.14
  (3 shorter events, 0.1 us)
Async XLA Ops:
  104.8 4.3 %copy-start = (f32[4,128]{1,0:T(4,128)S(1)}, f32[4,128]{1,0:T(4,128)}, u32[]{:S(2)}) copy-start(f32[4,128]{1,0:T(4,128)} %get-tuple-element.5) | copy-start | bytes 6148

commit v3 on v2

--- a/solution.py
+++ b/solution.py
@@ -137,13 +137,22 @@
 
     shards, wholes = (up_ref, down_ref), (up_all, down_all)
 
-    def rows(kind, xr, dist, cr):
+    up_pieces, down_pieces = (0, 1), (2, 3)
+
+    def rows(piece, xr, dist, cr):
+        kind, part = divmod(piece, 2)
         depth = shards[kind].shape[0]
         owner = member(xr, zs - dist, cr)
-        return wholes[kind].at[pl.ds(pl.multiple_of(owner * depth, depth), depth)]
-
-    def source(kind, xr, dist):
-        return shards[kind] if (xr, dist) == (0, 0) else rows(kind, xr, dist, 0)
+        start = pl.multiple_of(owner * depth + part * (depth // 2), depth // 2)
+        return wholes[kind].at[pl.ds(start, depth // 2)]
+
+    def own(piece):
+        kind, part = divmod(piece, 2)
+        depth = shards[kind].shape[0]
+        return shards[kind].at[pl.ds(part * (depth // 2), depth // 2)]
+
+    def source(piece, xr, dist):
+        return own(piece) if (xr, dist) == (0, 0) else rows(piece, xr, dist, 0)
 
     sent = []
 
@@ -151,73 +160,62 @@
         copy.start()
         sent.append(copy)
 
-    def send_half(kind):
-        send(remote(shards[kind], rows(kind, 0, 0, 0), half_send.at[kind], ring_recv.at[kind, 1, 0, 0], half))
-
-    def send_plus(kind, xr, dist):
+    def send_half(piece):
+        send(remote(own(piece), rows(piece, 0, 0, 0), half_send.at[piece], ring_recv.at[piece, 1, 0, 0], half))
+
+    def ring_send(piece, xr, dist, sems, dist_there, cr_there, device):
         send(
             remote(
-                source(kind, xr, dist),
-                rows(kind, xr, dist, 0),
-                plus_send.at[kind, xr, dist],
-                ring_recv.at[kind, xr, dist + 1, 0],
-                z_plus,
+                source(piece, xr, dist),
+                rows(piece, xr, dist, 0),
+                sems.at[piece, xr, dist],
+                ring_recv.at[piece, xr, dist_there, cr_there],
+                device,
             )
         )
 
-    def send_minus(kind, xr, dist):
-        send(
-            remote(
-                source(kind, xr, dist),
-                rows(kind, xr, dist, 0),
-                minus_send.at[kind, xr, dist],
-                ring_recv.at[kind, xr, (dist - 1) % zs, 0],
-                z_minus,
-            )
-        )
-
-    def send_core(kind, xr, dist):
-        send(
-            remote(
-                source(kind, xr, dist),
-                rows(kind, xr, dist, 0),
-                core_send.at[kind, xr, dist],
-                ring_recv.at[kind, xr, dist, 1],
-                sibling,
-            )
-        )
-
-    def arrived(kind, xr, dist, cr):
-        ref = rows(kind, xr, dist, cr)
-        remote(ref, ref, core_send.at[kind, xr, dist], ring_recv.at[kind, xr, dist, cr], sibling).wait_recv()
+    def send_plus(piece, xr, dist):
+        ring_send(piece, xr, dist, plus_send, dist + 1, 0, z_plus)
+
+    def send_minus(piece, xr, dist):
+        ring_send(piece, xr, dist, minus_send, (dist - 1) % zs, 0, z_minus)
+
+    def send_core(piece, xr, dist):
+        ring_send(piece, xr, dist, core_send, dist, 1, sibling)
+
+    def arrived(piece, xr, dist, cr):
+        ref = rows(piece, xr, dist, cr)
+        remote(ref, ref, core_send.at[piece, xr, dist], ring_recv.at[piece, xr, dist, cr], sibling).wait_recv()
 
     plus = (zs // 2, zs - 1 - zs // 2)
     minus = (zs - 1 - zs // 2, zs // 2)
     steps = zs // 2
 
-    def begin_own(kind):
-        send_plus(kind, 0, 0)
-        send_minus(kind, 0, 0)
-        send_core(kind, 0, 0)
-
-    def begin_half(kind):
-        arrived(kind, 1, 0, 0)
-        send_plus(kind, 1, 0)
-        send_minus(kind, 1, 0)
-        send_core(kind, 1, 0)
-
-    def ring_step(kind, step):
-        for xr in range(XHI):
-            if step <= plus[kind]:
-                arrived(kind, xr, step, 0)
-                if step < plus[kind]:
-                    send_plus(kind, xr, step)
-                send_core(kind, xr, step)
-            if step <= minus[kind]:
-                arrived(kind, xr, zs - step, 0)
-                if step < minus[kind]:
-                    send_minus(kind, xr, zs - step)
-                send_core(kind, xr, zs - step)
+    def begin(pieces_here, xr):
+        for piece in pieces_here:
+            if xr:
+                arrived(piece, xr, 0, 0)
+            send_plus(piece, xr, 0)
+            send_minus(piece, xr, 0)
+        for piece in pieces_here:
+            send_core(piece, xr, 0)
+
+    def ring_step(pieces_here, step, halves=(0, 1), between=None):
+        kind = pieces_here[0] // 2
+        for xr in halves:
+            for piece in pieces_here:
+                if step <= plus[kind]:
+                    arrived(piece, xr, step, 0)
+                    if step < plus[kind]:
+                        send_plus(piece, xr, step)
+                    send_core(piece, xr, step)
+                if step <= minus[kind]:
+                    arrived(piece, xr, zs - step, 0)
+                    if step < minus[kind]:
+                        send_minus(piece, xr, zs - step)
+                    send_core(piece, xr, zs - step)
+                if between is not None:
+                    between()
 
     own_columns = pl.ds(pl.multiple_of(core * half_columns, 128), half_columns)
     sibling_columns = pl.ds(pl.multiple_of((1 - core) * half_columns, 128), half_columns)
@@ -293,9 +291,12 @@
 
     for i in range(3):
         send(piece_copy(i))
-    send_half(0)
-    begin_own(0)
-    send_half(1)
+    for piece in up_pieces:
+        send_half(piece)
+    begin(up_pieces, 0)
+    for piece in down_pieces:
+        send_half(piece)
+    begin(down_pieces, 0)
 
     def fill(k):
         wanted = to_peer[k][0]
@@ -312,31 +313,47 @@
 
     for k in range(slots):
         fill(k)
-    dispatch(0)
-    dispatch(1)
+    early = slots // 2
+    for k in range(early):
+        dispatch(k)
 
     for kind in range(2):
         depth = shards[kind].shape[0]
         wholes[kind][pl.ds(pl.multiple_of(m * depth, depth), depth), :] = shards[kind][...]
 
+    total_rows = normed.shape[0]
+    part_rows = total_rows // 2
+    width = 256
+    up_parts = 2 * (up_all.shape[1] // width)
+    made = []
+
+    def up_part():
+        index = len(made)
+        if index >= up_parts:
+            return
+        made.append(index)
+        column_rows = pl.ds(index % 2 * part_rows, part_rows)
+        columns = pl.ds(index // 2 * width, width)
+        upward = jnp.dot(normed[column_rows, :], up_all[:, columns], preferred_element_type=jnp.float32)
+        active[column_rows, columns] = jax.nn.gelu(upward, approximate=True).astype(jnp.bfloat16)
+
     merge_pieces()
-    begin_half(0)
-    ring_step(0, 1)
+    begin(up_pieces, 1)
+    ring_step(up_pieces, 1)
     send_skips()
-    ring_step(0, 2)
+    begin(down_pieces, 1)
+    ring_step(up_pieces, 2)
     first_begin()
-    for k in range(2, local):
+    for k in range(early, local):
         dispatch(k)
+    ring_step(down_pieces, 1, (0,))
     for step in range(3, steps):
-        ring_step(0, step)
-    begin_own(1)
-    begin_half(1)
-    ring_step(0, steps)
+        ring_step(up_pieces, step)
+    ring_step(down_pieces, 1, (1,))
+    ring_step(up_pieces, steps)
     first_forward()
-    ring_step(1, 1)
+    ring_step(down_pieces, 2)
     second_begin()
-    for step in range(2, steps):
-        ring_step(1, step)
 
     for k in range(slots):
         if k != local:
@@ -344,38 +361,23 @@
         normed[pl.ds(k * BLOCK, BLOCK), :] = rms_scale(incoming[k].astype(jnp.float32), ng_ref[...]).astype(
             jnp.bfloat16
         )
-    for xr in range(XHI):
-        for dist in range(zs):
-            arrived(0, xr, dist, 1)
-
-    total_rows = normed.shape[0]
-    part_rows = total_rows // 2
-    width = 256
-    tiles = up_all.shape[1] // width
-
-    def up_tiles(first, last):
-        def one(i, carry):
-            col = pl.multiple_of(lax.div(i, 2) * width, width)
-            row = pl.multiple_of(lax.rem(i, 2) * part_rows, part_rows)
-            upward = jnp.dot(
-                normed[pl.ds(row, part_rows), :],
-                up_all[:, pl.ds(col, width)],
-                preferred_element_type=jnp.float32,
-            )
-            active[pl.ds(row, part_rows), pl.ds(col, width)] = jax.nn.gelu(upward, approximate=True).astype(
-                jnp.bfloat16
-            )
-            return carry
-
-        lax.fori_loop(2 * first, 2 * last, one, 0)
-
-    up_tiles(0, tiles // 2)
-    ring_step(1, steps)
+    for piece in up_pieces:
+        for xr in range(XHI):
+            for dist in range(zs):
+                arrived(piece, xr, dist, 1)
+
+    for step in range(3, steps):
+        ring_step(down_pieces, step, between=up_part)
+    for _ in range(up_parts // 4):
+        up_part()
+    ring_step(down_pieces, steps, between=up_part)
     second_forward()
-    up_tiles(tiles // 2, tiles)
-    for xr in range(XHI):
-        for dist in range(zs):
-            arrived(1, xr, dist, 1)
+    for _ in range(up_parts):
+        up_part()
+    for piece in down_pieces:
+        for xr in range(XHI):
+            for dist in range(zs):
+                arrived(piece, xr, dist, 1)
 
     def give_back(k):
         send(remote(hidden.at[k], returned.at[k], back_send.at[k], back_recv.at[k], from_peer[k]))
@@ -490,11 +492,11 @@
             pltpu.VMEM((slots, BLOCK, width), jnp.bfloat16),
             pltpu.VMEM((slots, 8, BLOCK), jnp.float32),
             pltpu.VMEM((slots, 8, BLOCK), jnp.float32),
-            dma((2, XHI, zs, CORES)),
-            dma((2, XHI, zs)),
-            dma((2, XHI, zs)),
-            dma((2, XHI, zs)),
-            dma((2,)),
+            dma((4, XHI, zs, CORES)),
+            dma((4, XHI, zs)),
+            dma((4, XHI, zs)),
+            dma((4, XHI, zs)),
+            dma((4,)),
             dma((slots,)),
             dma((slots,)),
             dma((slots,)),

time: 112 us -> 110 us (0.982)
    pallas_call x1, Pallas kernels: 102 us -> 101 us  [local(): pl.pallas_call(functools.partial(exchange_kernel, variants, members), out...]
where the time goes in v3:
time: 110 us; the launch traced here: 109 us
  Pallas kernels  101 us (92%)
  local copies, waits for them, and re-layouts  5.69 us (5%)
  between operations  1.32 us (1%)
    pallas_call x1, Pallas kernels, local(): pl.pallas_call(functools.partial(exchange_kernel, variants, members), out...  101 us
    unnamed x4, local copies, waits for them, and re-layouts  4.9 us

profile of v3, /device:TPU:8, one launch (start us, length us, event | category | flops | bytes accessed | tf_op | source)
XLA Modules:
  0.0 108.5 jit_solution(2739654199768323521)
XLA Ops:
  1.3 0.7 pad.4
  2.1 0.7 broadcast_select_fusion.piece_ref
  2.8 100.8 %exchange.1 = (bf16[512,2336]{1,0:T(8,128)(2,1)}, f32[4,128]{1,0:T(4,128)}) custom-call(s32[4]{0:T(128)} %bv_ref.1, bf16[512,1024]{1,0:T(8,128)(2,1)} %pos_ref.1, bf16[32,2048]{1,0:T(8,128)(2,1)} %bitcast.4, bf16[64,1024]{1,0:T(8,128)(2,1)} %bitcast.5, f32[1,1024]{1,0:T(1,128)} %ng_ref.1, f32[1,1024]{1,0:T(1,128)} %fg_ref.1, f32[1,1024]{1,0:T(1,128)} %vw_ref.1, ...), custom_call_target="tpu_custom_call" | custom-call | flops 8589934592 | bytes 8388608 | tf_op jit(solution)/shard_map/exchange/pallas_call | solution.py:474
  103.6 0.0 copy-start
  103.6 4.3 %copy.11 = bf16[512,2336]{0,1:T(8,128)(2,1)} copy(bf16[512,2336]{1,0:T(8,128)(2,1)} %get-tuple-element.6) | data formatting | bytes 4784128
  107.9 0.0 copy-done
  107.9 0.6 copy.14
  (3 shorter events, 0.1 us)
Async XLA Ops:
  103.6 4.3 %copy-start = (f32[4,128]{1,0:T(4,128)S(1)}, f32[4,128]{1,0:T(4,128)}, u32[]{:S(2)}) copy-start(f32[4,128]{1,0:T(4,128)} %get-tuple-element.5) | copy-start | bytes 6148

commit v4 on v3

--- a/solution.py
+++ b/solution.py
@@ -36,7 +36,7 @@
     fg_ref,
     vw_ref,
     count_ref,
-    piece_ref,
+    rows_ref,
     policy_out,
     val_out,
     outgoing,
@@ -60,7 +60,7 @@
     back_recv,
     value_send,
     value_recv,
-    own_hidden,
+    piece_ref,
     policy_all,
     pieces,
     piece_send,
@@ -129,11 +129,9 @@
         return policy_rows(0, 0, 0, lax.div(lax.rem(z + dz, zs), 2) * tile_rows, tile_rows)
 
     barrier = pltpu.get_barrier_semaphore()
-    greeted = [z_plus, z_minus, sibling, half, *to_peer[:local]]
-    greeted += [other_z_sibling, (peer(0, 1), member(1, 0, 0)), *skip_to]
+    greeted = [z_plus, z_minus, sibling, half, *to_peer[:local], other_z_sibling, (peer(0, 1), member(1, 0, 0)), *skip_to]
     for device in greeted:
         pl.semaphore_signal(barrier, inc=1, device_id=device, device_id_type=MESH)
-    pl.semaphore_wait(barrier, len(greeted))
 
     shards, wholes = (up_ref, down_ref), (up_all, down_all)
 
@@ -289,15 +287,6 @@
             second_copy(a, 2, 2).wait_recv()
             policy_to_core(a, 2)
 
-    for i in range(3):
-        send(piece_copy(i))
-    for piece in up_pieces:
-        send_half(piece)
-    begin(up_pieces, 0)
-    for piece in down_pieces:
-        send_half(piece)
-    begin(down_pieces, 0)
-
     def fill(k):
         wanted = to_peer[k][0]
         block = pos_ref[0:BLOCK, :]
@@ -311,9 +300,29 @@
     def dispatch(k):
         send(remote(outgoing.at[k], incoming.at[k], slot_send.at[k], slot_recv.at[k], to_peer[k]))
 
+    rows_here, moves = rows_ref.shape
+    place = lax.rem(m, tile_rows // rows_here) * rows_here
+    spread = lax.broadcasted_iota(jnp.int32, (tile_rows, rows_here), 0) == place + lax.broadcasted_iota(
+        jnp.int32, (tile_rows, rows_here), 1
+    )
+    piece_ref[...] = jnp.zeros(piece_ref.shape, jnp.bfloat16)
+    piece_ref[:, :moves] = jnp.dot(
+        spread.astype(jnp.bfloat16), rows_ref[...], preferred_element_type=jnp.float32
+    ).astype(jnp.bfloat16)
     for k in range(slots):
         fill(k)
-    early = slots // 2
+
+    pl.semaphore_wait(barrier, len(greeted))
+    for i in range(3):
+        send(piece_copy(i))
+    for piece in up_pieces:
+        send_half(piece)
+    begin(up_pieces, 0)
+    for piece in down_pieces:
+        send_half(piece)
+    begin(down_pieces, 0)
+
+    early = slots // 4
     for k in range(early):
         dispatch(k)
 
@@ -337,23 +346,26 @@
         upward = jnp.dot(normed[column_rows, :], up_all[:, columns], preferred_element_type=jnp.float32)
         active[column_rows, columns] = jax.nn.gelu(upward, approximate=True).astype(jnp.bfloat16)
 
+    middle = slots // 2
     merge_pieces()
     begin(up_pieces, 1)
+    begin(down_pieces, 1)
+    send_skips()
     ring_step(up_pieces, 1)
-    send_skips()
-    begin(down_pieces, 1)
+    first_begin()
+    for k in range(early, middle):
+        dispatch(k)
     ring_step(up_pieces, 2)
-    first_begin()
-    for k in range(early, local):
+    first_forward()
+    for k in range(middle, local):
         dispatch(k)
     ring_step(down_pieces, 1, (0,))
     for step in range(3, steps):
         ring_step(up_pieces, step)
     ring_step(down_pieces, 1, (1,))
+    second_begin()
     ring_step(up_pieces, steps)
-    first_forward()
     ring_step(down_pieces, 2)
-    second_begin()
 
     for k in range(slots):
         if k != local:
@@ -368,10 +380,10 @@
 
     for step in range(3, steps):
         ring_step(down_pieces, step, between=up_part)
-    for _ in range(up_parts // 4):
+    for _ in range(up_parts // 2):
         up_part()
+    second_forward()
     ring_step(down_pieces, steps, between=up_part)
-    second_forward()
     for _ in range(up_parts):
         up_part()
     for piece in down_pieces:
@@ -399,46 +411,50 @@
                 give_back(k)
 
     second_end()
-    for k in range(slots):
+    for a in range(xs):
+        for b in range(ys):
+            ref = policy_rows(a, b, 1)
+            remote(ref, ref, policy_core_send.at[a, b], policy_core_recv.at[a, b], sibling).wait_recv()
+
+    count = count_ref[0]
+    blocks = bv_ref.shape[0]
+    games = lax.broadcasted_iota(jnp.int32, (1, BLOCK), 1)
+    whole_tiles = moves // width
+    rest = moves - whole_tiles * width
+
+    def slot_logits(k, keep, columns, count_rows, row, fresh):
+        logits = jnp.dot(returned[k], policy_all[:, columns], preferred_element_type=jnp.float32)
+        turned = jnp.transpose(logits.astype(jnp.bfloat16))[:count_rows]
+        for b in range(blocks):
+            place = (pl.ds(row, count_rows), pl.ds(b * BLOCK, BLOCK))
+            part = turned * keep[b]
+            policy_out[place] = part if fresh else policy_out[place] + part
+
+    for position, k in enumerate([local, *range(local)]):
         if k != local:
             remote(hidden.at[k], returned.at[k], back_send.at[k], back_recv.at[k], from_peer[k]).wait_recv()
             remote(
                 estimate.at[k], estimate_back.at[k], value_send.at[k], value_recv.at[k], from_peer[k]
             ).wait_recv()
-    for a in range(xs):
-        for b in range(ys):
-            ref = policy_rows(a, b, 1)
-            remote(ref, ref, policy_core_send.at[a, b], policy_core_recv.at[a, b], sibling).wait_recv()
-
-    count = count_ref[0]
-    for b in range(bv_ref.shape[0]):
-        block, value = returned[0], estimate_back[0]
+        keep = [
+            jnp.where((games + b * BLOCK < count) & (bv_ref[b] == to_peer[k][0]), 1.0, 0.0).astype(jnp.bfloat16)
+            for b in range(blocks)
+        ]
+
+        def step_of(i, carry):
+            row = pl.multiple_of(i * width, width)
+            slot_logits(k, keep, pl.ds(row, width), width, row, position == 0)
+            return carry
+
+        lax.fori_loop(0, whole_tiles, step_of, 0)
+        if rest:
+            slot_logits(k, keep, pl.ds(whole_tiles * width, width), rest, whole_tiles * width, position == 0)
+
+    for b in range(blocks):
+        value = estimate_back[0]
         for k in range(1, slots):
-            chosen = bv_ref[b] == to_peer[k][0]
-            block = jnp.where(chosen, returned[k], block)
-            value = jnp.where(chosen, estimate_back[k], value)
-        own_hidden[pl.ds(b * BLOCK, BLOCK), :] = block
-        games = b * BLOCK + lax.broadcasted_iota(jnp.int32, (1, BLOCK), 1)
-        val_out[pl.ds(b, 1), :] = jnp.where(games < count, value[0:1], 0.0)
-
-    games_here, moves = policy_out.shape
-    live = lax.broadcasted_iota(jnp.int32, (games_here, 1), 0) < count
-
-    def masked_logits(columns):
-        logits = jnp.dot(own_hidden[...], policy_all[:, columns], preferred_element_type=jnp.float32)
-        return jnp.where(live, logits, 0.0).astype(jnp.bfloat16)
-
-    whole_tiles = moves // width
-
-    def policy_tile_step(i, carry):
-        columns = pl.ds(pl.multiple_of(i * width, width), width)
-        policy_out[:, columns] = masked_logits(columns)
-        return carry
-
-    lax.fori_loop(0, whole_tiles, policy_tile_step, 0)
-    rest = moves - whole_tiles * width
-    if rest:
-        policy_out[:, pl.ds(whole_tiles * width, rest)] = masked_logits(pl.ds(whole_tiles * width, width))[:, :rest]
+            value = jnp.where(bv_ref[b] == to_peer[k][0], estimate_back[k], value)
+        val_out[pl.ds(b, 1), :] = jnp.where(games + b * BLOCK < count, value[0:1], 0.0)
 
     for copy in sent:
         copy.wait_send()
@@ -467,14 +483,10 @@
     policy_rows_here, moves = policy_weight.shape
     half_columns = -(-moves // (CORES * 128)) * 128
     tile_rows = 2 * CORES * policy_rows_here
-    widened = jnp.pad(policy_weight, ((0, 0), (0, CORES * half_columns - moves)))
-    place = lax.rem(lax.axis_index("mp"), 2 * CORES)
-    in_place = lax.div(jnp.arange(tile_rows, dtype=jnp.int32), policy_rows_here) == place
-    piece = jnp.where(in_place[:, None], jnp.tile(widened, (2 * CORES, 1)), jnp.zeros((), jnp.bfloat16))
     policy, value = pl.pallas_call(
         functools.partial(exchange_kernel, variants, members),
         out_shape=(
-            jax.ShapeDtypeStruct((games_here, moves), jnp.bfloat16),
+            jax.ShapeDtypeStruct((moves, games_here), jnp.bfloat16),
             jax.ShapeDtypeStruct((blocks, BLOCK), jnp.float32),
         ),
         in_specs=[pl.BlockSpec(memory_space=pltpu.SMEM)]
@@ -503,7 +515,7 @@
             dma((slots,)),
             dma((slots,)),
             dma((slots,)),
-            pltpu.VMEM((games_here, width), jnp.bfloat16),
+            pltpu.VMEM((tile_rows, CORES * half_columns), jnp.bfloat16),
             pltpu.VMEM((variants * members * policy_rows_here, CORES * half_columns), jnp.bfloat16),
             pltpu.VMEM((3, tile_rows, half_columns), jnp.bfloat16),
             dma((3,)),
@@ -533,9 +545,9 @@
         final_gain,
         value_weight,
         game_counts,
-        piece,
+        policy_weight,
     )
-    return (policy, value.reshape(games_here))
+    return (policy.T, value.reshape(games_here))
 
 
 def solution(mesh):

time: 110 us -> 115 us (1.045); the launches traced: 109 us -> 115 us
  Pallas kernels: 101 us -> 110 us
  local copies, waits for them, and re-layouts: 5.69 us -> 3.83 us
    pallas_call x1, Pallas kernels: 101 us -> 110 us  [local(): pl.pallas_call(functools.partial(exchange_kernel, variants, members), out...]
where the time goes in v4:
time: 115 us
  Pallas kernels  110 us (96%)
  local copies, waits for them, and re-layouts  3.83 us (3%)
  between operations  1.3 us (1%)
    pallas_call x1, Pallas kernels, local(): pl.pallas_call(functools.partial(exchange_kernel, variants, members), out...  110 us
    unnamed x4, local copies, waits for them, and re-layouts  3.83 us

profile of v4, /device:TPU:8, one launch (start us, length us, event | category | flops | bytes accessed | tf_op | source)
XLA Modules:
  0.0 115.3 jit_solution(15414953626637608364)
XLA Ops:
  1.3 110.2 %exchange.1 = (bf16[2336,512]{1,0:T(8,128)(2,1)}, f32[4,128]{1,0:T(4,128)}) custom-call(s32[4]{0:T(128)} %bv_ref.1, bf16[512,1024]{1,0:T(8,128)(2,1)} %pos_ref.1, bf16[32,2048]{1,0:T(8,128)(2,1)} %bitcast.6, bf16[64,1024]{1,0:T(8,128)(2,1)} %bitcast.7, f32[1,1024]{1,0:T(1,128)} %ng_ref.1, f32[1,1024]{1,0:T(1,128)} %fg_ref.1, f32[1,1024]{1,0:T(1,128)} %vw_ref.1, ...), custom_call_target="tpu_custom_call" | custom-call | flops 8589934592 | bytes 8388608 | tf_op jit(solution)/shard_map/exchange/pallas_call | solution.py:486
  111.5 0.0 copy-start
  111.5 3.2 %copy.14 = bf16[512,2336]{0,1:T(8,128)(2,1)} copy(bf16[512,2336]{0,1:T(8,128)(2,1)} %bitcast.4) | data formatting | bytes 4784128
  114.7 0.0 copy-done
  114.7 0.6 copy.15
Async XLA Ops:
  111.5 3.3 %copy-start = (f32[4,128]{1,0:T(4,128)S(1)}, f32[4,128]{1,0:T(4,128)}, u32[]{:S(2)}) copy-start(f32[4,128]{1,0:T(4,128)} %get-tuple-element.5) | copy-start | bytes 6148

commit v5 on v3

--- a/solution.py
+++ b/solution.py
@@ -36,7 +36,7 @@
     fg_ref,
     vw_ref,
     count_ref,
-    piece_ref,
+    rows_ref,
     policy_out,
     val_out,
     outgoing,
@@ -61,6 +61,7 @@
     value_send,
     value_recv,
     own_hidden,
+    piece_ref,
     policy_all,
     pieces,
     piece_send,
@@ -100,7 +101,6 @@
     unit_rows = zs // 2 * tile_rows
     paired = z + 1 - 2 * lax.rem(z, 2) - z
     other_z = (v, member(0, zs + paired, 0))
-    other_z_sibling = (v, member(0, zs + paired, 1))
     x = xh * XLO + xl
     xs = XHI * XLO
 
@@ -113,8 +113,7 @@
 
     first_plus, first_minus = chip(*along(1, 0)), chip(*along(3, 0))
     second_plus, second_minus = chip(*along(0, 1)), chip(*along(0, 3))
-    skips = (2, zs - 2, zs // 2)
-    skip_to = [(v, member(0, d, 0)) for d in skips]
+    out_z = (v, member(0, zs - paired, 0))
 
     def policy_rows(a, b, cr, start=0, count=None):
         axis = lax.rem(core + cr, CORES)
@@ -129,11 +128,9 @@
         return policy_rows(0, 0, 0, lax.div(lax.rem(z + dz, zs), 2) * tile_rows, tile_rows)
 
     barrier = pltpu.get_barrier_semaphore()
-    greeted = [z_plus, z_minus, sibling, half, *to_peer[:local]]
-    greeted += [other_z_sibling, (peer(0, 1), member(1, 0, 0)), *skip_to]
+    greeted = [z_plus, z_minus, sibling, half, *to_peer[:local], (peer(0, 1), member(1, 0, 0))]
     for device in greeted:
         pl.semaphore_signal(barrier, inc=1, device_id=device, device_id_type=MESH)
-    pl.semaphore_wait(barrier, len(greeted))
 
     shards, wholes = (up_ref, down_ref), (up_all, down_all)
 
@@ -221,24 +218,30 @@
     sibling_columns = pl.ds(pl.multiple_of((1 - core) * half_columns, 128), half_columns)
 
     def piece_copy(i):
-        columns = own_columns if i == 1 else sibling_columns
-        device = (sibling, other_z, other_z_sibling)[i]
-        return remote(piece_ref.at[:, columns], pieces.at[i], piece_send.at[i], piece_recv.at[i], device)
-
-    def merge_pieces():
-        total = piece_ref[:, own_columns].astype(jnp.float32)
-        for i in range(3):
-            piece_copy(i).wait_recv()
-            total = total + pieces[i].astype(jnp.float32)
+        source_ref = piece_ref.at[:, sibling_columns] if i == 0 else pieces.at[2]
+        return remote(source_ref, pieces.at[i], piece_send.at[i], piece_recv.at[i], (sibling, other_z)[i])
+
+    def merge_chip():
+        piece_copy(0).wait_recv()
+        mine = piece_ref[:, own_columns].astype(jnp.float32)
+        pieces[2] = (mine + pieces[0].astype(jnp.float32)).astype(jnp.bfloat16)
+
+    def merge_pair():
+        piece_copy(1).wait_recv()
+        total = pieces[2].astype(jnp.float32) + pieces[1].astype(jnp.float32)
         policy_tile(0)[...] = total.astype(jnp.bfloat16)
 
-    def skip_copy(i, dz):
+    hop_sent = (0, zs - paired, 2 * zs + 2 * paired)
+    hop_got = (zs - paired, 2 * zs + 2 * paired, 3 * zs - 3 * paired)
+
+    def hop_copy(i, dz):
         ref = policy_tile(dz)
-        return remote(ref, ref, pair_send.at[i], pair_recv.at[i], skip_to[i])
-
-    def send_skips():
-        for i in range(len(skips)):
-            send(skip_copy(i, 0))
+        return remote(ref, ref, pair_send.at[i], pair_recv.at[i], (out_z, other_z, out_z)[i])
+
+    def hop_send(i):
+        if i:
+            hop_copy(i - 1, hop_got[i - 1]).wait_recv()
+        send(hop_copy(i, hop_sent[i]))
 
     def policy_to_core(a, b):
         ref = policy_rows(a, b, 0)
@@ -251,8 +254,7 @@
         return remote(ref, ref, first_send.at[i], first_recv.at[i], (first_plus, first_minus)[i % 2])
 
     def first_begin():
-        for i, dz in enumerate(skips):
-            skip_copy(i, zs - dz).wait_recv()
+        hop_copy(2, hop_got[2]).wait_recv()
         send(first_copy(0, 0))
         send(first_copy(1, 0))
         policy_to_core(0, 0)
@@ -288,15 +290,6 @@
         for a in range(xs):
             second_copy(a, 2, 2).wait_recv()
             policy_to_core(a, 2)
-
-    for i in range(3):
-        send(piece_copy(i))
-    for piece in up_pieces:
-        send_half(piece)
-    begin(up_pieces, 0)
-    for piece in down_pieces:
-        send_half(piece)
-    begin(down_pieces, 0)
 
     def fill(k):
         wanted = to_peer[k][0]
@@ -311,15 +304,33 @@
     def dispatch(k):
         send(remote(outgoing.at[k], incoming.at[k], slot_send.at[k], slot_recv.at[k], to_peer[k]))
 
+    rows_here, moves = rows_ref.shape
+    place = lax.rem(m, tile_rows // rows_here) * rows_here
+    spread = lax.broadcasted_iota(jnp.int32, (tile_rows, rows_here), 0) == place + lax.broadcasted_iota(
+        jnp.int32, (tile_rows, rows_here), 1
+    )
+    piece_ref[...] = jnp.zeros(piece_ref.shape, jnp.bfloat16)
+    piece_ref[:, :moves] = jnp.dot(
+        spread.astype(jnp.bfloat16), rows_ref[...], preferred_element_type=jnp.float32
+    ).astype(jnp.bfloat16)
     for k in range(slots):
         fill(k)
-    early = slots // 2
-    for k in range(early):
+
+    pl.semaphore_wait(barrier, len(greeted))
+    send(piece_copy(0))
+    for piece in (*up_pieces, *down_pieces):
+        send_half(piece)
+    begin(up_pieces, 0)
+    for k in range(local):
         dispatch(k)
+    merge_chip()
 
     for kind in range(2):
         depth = shards[kind].shape[0]
         wholes[kind][pl.ds(pl.multiple_of(m * depth, depth), depth), :] = shards[kind][...]
+
+    send(piece_copy(1))
+    begin(down_pieces, 0)
 
     total_rows = normed.shape[0]
     part_rows = total_rows // 2
@@ -337,23 +348,23 @@
         upward = jnp.dot(normed[column_rows, :], up_all[:, columns], preferred_element_type=jnp.float32)
         active[column_rows, columns] = jax.nn.gelu(upward, approximate=True).astype(jnp.bfloat16)
 
-    merge_pieces()
     begin(up_pieces, 1)
+    merge_pair()
+    begin(down_pieces, 1)
+    hop_send(0)
     ring_step(up_pieces, 1)
-    send_skips()
-    begin(down_pieces, 1)
+    ring_step(down_pieces, 1, (0,))
+    hop_send(1)
     ring_step(up_pieces, 2)
-    first_begin()
-    for k in range(early, local):
-        dispatch(k)
-    ring_step(down_pieces, 1, (0,))
+    hop_send(2)
     for step in range(3, steps):
         ring_step(up_pieces, step)
     ring_step(down_pieces, 1, (1,))
+    first_begin()
     ring_step(up_pieces, steps)
+    ring_step(down_pieces, 2, (0,))
     first_forward()
-    ring_step(down_pieces, 2)
-    second_begin()
+    ring_step(down_pieces, 2, (1,))
 
     for k in range(slots):
         if k != local:
@@ -366,12 +377,14 @@
             for dist in range(zs):
                 arrived(piece, xr, dist, 1)
 
-    for step in range(3, steps):
+    ring_step(down_pieces, 3, (0,), up_part)
+    second_begin()
+    ring_step(down_pieces, 3, (1,), up_part)
+    for step in range(4, steps):
         ring_step(down_pieces, step, between=up_part)
-    for _ in range(up_parts // 4):
+    for _ in range(up_parts // 2):
         up_part()
     ring_step(down_pieces, steps, between=up_part)
-    second_forward()
     for _ in range(up_parts):
         up_part()
     for piece in down_pieces:
@@ -397,6 +410,8 @@
         for k in range(first, first + GROUP):
             if k != local:
                 give_back(k)
+        if first == 0:
+            second_forward()
 
     second_end()
     for k in range(slots):
@@ -421,7 +436,7 @@
         games = b * BLOCK + lax.broadcasted_iota(jnp.int32, (1, BLOCK), 1)
         val_out[pl.ds(b, 1), :] = jnp.where(games < count, value[0:1], 0.0)
 
-    games_here, moves = policy_out.shape
+    games_here = policy_out.shape[0]
     live = lax.broadcasted_iota(jnp.int32, (games_here, 1), 0) < count
 
     def masked_logits(columns):
@@ -467,10 +482,6 @@
     policy_rows_here, moves = policy_weight.shape
     half_columns = -(-moves // (CORES * 128)) * 128
     tile_rows = 2 * CORES * policy_rows_here
-    widened = jnp.pad(policy_weight, ((0, 0), (0, CORES * half_columns - moves)))
-    place = lax.rem(lax.axis_index("mp"), 2 * CORES)
-    in_place = lax.div(jnp.arange(tile_rows, dtype=jnp.int32), policy_rows_here) == place
-    piece = jnp.where(in_place[:, None], jnp.tile(widened, (2 * CORES, 1)), jnp.zeros((), jnp.bfloat16))
     policy, value = pl.pallas_call(
         functools.partial(exchange_kernel, variants, members),
         out_shape=(
@@ -504,6 +515,7 @@
             dma((slots,)),
             dma((slots,)),
             pltpu.VMEM((games_here, width), jnp.bfloat16),
+            pltpu.VMEM((tile_rows, CORES * half_columns), jnp.bfloat16),
             pltpu.VMEM((variants * members * policy_rows_here, CORES * half_columns), jnp.bfloat16),
             pltpu.VMEM((3, tile_rows, half_columns), jnp.bfloat16),
             dma((3,)),
@@ -533,7 +545,7 @@
         final_gain,
         value_weight,
         game_counts,
-        piece,
+        policy_weight,
     )
     return (policy, value.reshape(games_here))
 

time: 110 us -> 107 us (0.973)
  Pallas kernels: 101 us -> 99.8 us
where the time goes in v5:
time: 107 us; the launch traced here: 106 us
  Pallas kernels  99.8 us (93%)
  local copies, waits for them, and re-layouts  4.9 us (5%)
  between operations  1.3 us (1%)
    pallas_call x1, Pallas kernels, local(): pl.pallas_call(functools.partial(exchange_kernel, variants, members), out...  99.8 us
    unnamed x4, local copies, waits for them, and re-layouts  4.9 us

profile of v5, /device:TPU:8, one launch (start us, length us, event | category | flops | bytes accessed | tf_op | source)
XLA Modules:
  0.0 106.0 jit_solution(1255848349225934208)
XLA Ops:
  1.3 99.8 %exchange.1 = (bf16[512,2336]{1,0:T(8,128)(2,1)}, f32[4,128]{1,0:T(4,128)}) custom-call(s32[4]{0:T(128)} %bv_ref.1, bf16[512,1024]{1,0:T(8,128)(2,1)} %pos_ref.1, bf16[32,2048]{1,0:T(8,128)(2,1)} %bitcast.4, bf16[64,1024]{1,0:T(8,128)(2,1)} %bitcast.5, f32[1,1024]{1,0:T(1,128)} %ng_ref.1, f32[1,1024]{1,0:T(1,128)} %fg_ref.1, f32[1,1024]{1,0:T(1,128)} %vw_ref.1, ...), custom_call_target="tpu_custom_call" | custom-call | flops 8589934592 | bytes 8388608 | tf_op jit(solution)/shard_map/exchange/pallas_call | solution.py:485
  101.1 0.0 copy-start
  101.1 4.3 %copy.11 = bf16[512,2336]{0,1:T(8,128)(2,1)} copy(bf16[512,2336]{1,0:T(8,128)(2,1)} %get-tuple-element.6) | data formatting | bytes 4784128
  105.4 0.0 copy-done
  105.4 0.6 copy.14
Async XLA Ops:
  101.1 4.3 %copy-start = (f32[4,128]{1,0:T(4,128)S(1)}, f32[4,128]{1,0:T(4,128)}, u32[]{:S(2)}) copy-start(f32[4,128]{1,0:T(4,128)} %get-tuple-element.5) | copy-start | bytes 6148

commit v6 on v5

--- a/solution.py
+++ b/solution.py
@@ -257,12 +257,14 @@
         hop_copy(2, hop_got[2]).wait_recv()
         send(first_copy(0, 0))
         send(first_copy(1, 0))
+        second_send_rows(0)
         policy_to_core(0, 0)
 
     def first_forward():
         for i, a in ((0, 1), (1, 3)):
             first_copy(i, a).wait_recv()
             send(first_copy(2 + i, a))
+            second_send_rows(a)
             policy_to_core(a, 0)
 
     def second_copy(a, i, b):
@@ -273,10 +275,12 @@
     def second_begin():
         for i in (2, 3):
             first_copy(i, 2).wait_recv()
+        second_send_rows(2)
         policy_to_core(2, 0)
-        for a in range(xs):
-            send(second_copy(a, 0, 0))
-            send(second_copy(a, 1, 0))
+
+    def second_send_rows(a):
+        send(second_copy(a, 0, 0))
+        send(second_copy(a, 1, 0))
 
     def second_forward():
         for a in range(xs):
@@ -348,10 +352,10 @@
         upward = jnp.dot(normed[column_rows, :], up_all[:, columns], preferred_element_type=jnp.float32)
         active[column_rows, columns] = jax.nn.gelu(upward, approximate=True).astype(jnp.bfloat16)
 
+    merge_pair()
     begin(up_pieces, 1)
-    merge_pair()
+    hop_send(0)
     begin(down_pieces, 1)
-    hop_send(0)
     ring_step(up_pieces, 1)
     ring_step(down_pieces, 1, (0,))
     hop_send(1)
@@ -384,6 +388,7 @@
         ring_step(down_pieces, step, between=up_part)
     for _ in range(up_parts // 2):
         up_part()
+    second_forward()
     ring_step(down_pieces, steps, between=up_part)
     for _ in range(up_parts):
         up_part()
@@ -410,8 +415,6 @@
         for k in range(first, first + GROUP):
             if k != local:
                 give_back(k)
-        if first == 0:
-            second_forward()
 
     second_end()
     for k in range(slots):

time: 107 us -> 106 us (level); the launches traced: 106 us -> 104 us
  Pallas kernels: 99.8 us -> 97.5 us
    pallas_call x1, Pallas kernels: 99.8 us -> 97.5 us  [local(): pl.pallas_call(functools.partial(exchange_kernel, variants, members), out...]
where the time goes in v6:
time: 106 us; the launch traced here: 104 us
  Pallas kernels  97.5 us (92%)
  local copies, waits for them, and re-layouts  4.9 us (5%)
  between operations  1.3 us (1%)
    pallas_call x1, Pallas kernels, local(): pl.pallas_call(functools.partial(exchange_kernel, variants, members), out...  97.5 us
    unnamed x4, local copies, waits for them, and re-layouts  4.9 us

profile of v6, /device:TPU:8, one launch (start us, length us, event | category | flops | bytes accessed | tf_op | source)
XLA Modules:
  0.0 103.7 jit_solution(13711592139529157703)
XLA Ops:
  1.3 97.5 %exchange.1 = (bf16[512,2336]{1,0:T(8,128)(2,1)}, f32[4,128]{1,0:T(4,128)}) custom-call(s32[4]{0:T(128)} %bv_ref.1, bf16[512,1024]{1,0:T(8,128)(2,1)} %pos_ref.1, bf16[32,2048]{1,0:T(8,128)(2,1)} %bitcast.4, bf16[64,1024]{1,0:T(8,128)(2,1)} %bitcast.5, f32[1,1024]{1,0:T(1,128)} %ng_ref.1, f32[1,1024]{1,0:T(1,128)} %fg_ref.1, f32[1,1024]{1,0:T(1,128)} %vw_ref.1, ...), custom_call_target="tpu_custom_call" | custom-call | flops 8589934592 | bytes 8388608 | tf_op jit(solution)/shard_map/exchange/pallas_call | solution.py:488
  98.8 0.0 copy-start
  98.8 4.3 %copy.11 = bf16[512,2336]{0,1:T(8,128)(2,1)} copy(bf16[512,2336]{1,0:T(8,128)(2,1)} %get-tuple-element.6) | data formatting | bytes 4784128
  103.1 0.0 copy-done
  103.1 0.6 copy.14
Async XLA Ops:
  98.8 4.3 %copy-start = (f32[4,128]{1,0:T(4,128)S(1)}, f32[4,128]{1,0:T(4,128)}, u32[]{:S(2)}) copy-start(f32[4,128]{1,0:T(4,128)} %get-tuple-element.5) | copy-start | bytes 6148

commit v7 on v6

--- a/solution.py
+++ b/solution.py
@@ -282,8 +282,8 @@
         send(second_copy(a, 0, 0))
         send(second_copy(a, 1, 0))
 
-    def second_forward():
-        for a in range(xs):
+    def second_forward(groups):
+        for a in groups:
             for i, b in ((0, 1), (1, 3)):
                 second_copy(a, i, b).wait_recv()
                 if (i == 0) == (a < 2):
@@ -381,15 +381,14 @@
             for dist in range(zs):
                 arrived(piece, xr, dist, 1)
 
-    ring_step(down_pieces, 3, (0,), up_part)
     second_begin()
-    ring_step(down_pieces, 3, (1,), up_part)
-    for step in range(4, steps):
+    for step in range(3, steps):
         ring_step(down_pieces, step, between=up_part)
     for _ in range(up_parts // 2):
         up_part()
-    second_forward()
+    second_forward((0, 1, 3))
     ring_step(down_pieces, steps, between=up_part)
+    second_forward((2,))
     for _ in range(up_parts):
         up_part()
     for piece in down_pieces:

time: 106 us -> 105 us (level)
  no operation moved by 1% of the time
where the time goes in v7:
time: 105 us; the launch traced here: 103 us
  Pallas kernels  96.9 us (92%)
  local copies, waits for them, and re-layouts  4.9 us (5%)
  between operations  1.3 us (1%)
    pallas_call x1, Pallas kernels, local(): pl.pallas_call(functools.partial(exchange_kernel, variants, members), out...  96.9 us
    unnamed x4, local copies, waits for them, and re-layouts  4.9 us

profile of v7, /device:TPU:8, one launch (start us, length us, event | category | flops | bytes accessed | tf_op | source)
XLA Modules:
  0.0 103.1 jit_solution(11407749076273505151)
XLA Ops:
  1.3 96.9 %exchange.1 = (bf16[512,2336]{1,0:T(8,128)(2,1)}, f32[4,128]{1,0:T(4,128)}) custom-call(s32[4]{0:T(128)} %bv_ref.1, bf16[512,1024]{1,0:T(8,128)(2,1)} %pos_ref.1, bf16[32,2048]{1,0:T(8,128)(2,1)} %bitcast.4, bf16[64,1024]{1,0:T(8,128)(2,1)} %bitcast.5, f32[1,1024]{1,0:T(1,128)} %ng_ref.1, f32[1,1024]{1,0:T(1,128)} %fg_ref.1, f32[1,1024]{1,0:T(1,128)} %vw_ref.1, ...), custom_call_target="tpu_custom_call" | custom-call | flops 8589934592 | bytes 8388608 | tf_op jit(solution)/shard_map/exchange/pallas_call | solution.py:487
  98.2 0.0 copy-start
  98.2 4.3 %copy.11 = bf16[512,2336]{0,1:T(8,128)(2,1)} copy(bf16[512,2336]{1,0:T(8,128)(2,1)} %get-tuple-element.6) | data formatting | bytes 4784128
  102.6 0.0 copy-done
  102.6 0.6 copy.14
Async XLA Ops:
  98.2 4.3 %copy-start = (f32[4,128]{1,0:T(4,128)S(1)}, f32[4,128]{1,0:T(4,128)}, u32[]{:S(2)}) copy-start(f32[4,128]{1,0:T(4,128)} %get-tuple-element.5) | copy-start | bytes 6148
